TPU v7x, 1024 devices: a whole 4x8x16 slice. The times are simulated.
1024 devices in a mesh: gy: 64 (over y, x, core), gx: 16 (over z).
Axes of the slice: x: 4, y: 8, z: 16, core: 2. Of those that a mesh axis runs over, the one named last changes fastest.
Arguments:
- fields: bfloat16 [16, 1472, 2048], P(None, 'gy', 'gx'), may hold values from -6 to 6
- level_order: int32 [16], replicated, may hold values from 0 to 15, each once
- m_owner: int32 [1024], replicated, may hold values from 0 to 63, as said below
- n_count: int32 [1024], replicated, may hold values from 1 to 736, as said below
Outputs:
- spectrum: float32 [16, 1536, 2944], P('gx', 'gy')
Inputs may be any that keep to these rules, and one draw needn't show every extreme that they name: `m_owner`: each owner is named by at most 24 wavenumbers m, and some owner by exactly 24. Wavenumbers n = 0 to n_count[m] - 1 are retained for m; the count for m = 0 is 736.
All inputs are finite; a program needn't handle non-finite values.
Results may differ from a plain program's by a relative error of at most 0.0066.
Values may be sent and summed in bfloat16 or wider, within the bound.
No kernel may reach another device: no remote copies, remote signals or barrier semaphores. Data moves between devices by JAX's collectives and lax.ppermute only.
A program may use at most 32 MiB of HBM per device.

v0:
```python
import math

import jax
import jax.numpy as jnp
import numpy as np
from jax import lax
from jax.experimental import pallas as pl
from jax.experimental.pallas import tpu as pltpu
from jax.sharding import PartitionSpec as P

NX = 2048
NY = 1472
M = 1024
NN = 736
MCAP = 24
N_GY = 64
N_GX = 16
ROWS_Y = 23
LANE = 128
KX = M + LANE + M
F32 = jnp.float32
BF16 = jnp.bfloat16


def mode_tables(extent, mode_total):
    middle = extent // 2
    points = np.arange(middle + 1, dtype=np.int64)
    orders = np.arange(mode_total, dtype=np.int64)
    phases = (points[:, None] * orders[None, :] % extent).astype(np.float32) * np.float32(
        2.0 * math.pi / extent
    )
    weight = np.where((points == 0) | (points == middle), 0.5, 1.0).astype(np.float32)
    factor = np.float32(1.0 / math.sqrt(extent))
    cos_even = weight[:, None] * np.cos(phases) * factor
    sin_odd = -np.sin(phases) * factor
    return cos_even, sin_odd


def x_table():
    cos_x, sin_x = mode_tables(NX, M)
    table = np.zeros((M, KX), np.float32)
    table[:, : M + 1] = cos_x.T
    table[:, M + LANE :] = sin_x[:M].T
    return table.astype(BF16)


def y_tables():
    cos_y, sin_y = mode_tables(NY, NN)
    half = N_GY // 2
    cos_rows = np.zeros((half, 32, 768), np.float32)
    sin_rows = np.zeros((half, 32, 896), np.float32)
    cos_rows[:, :ROWS_Y, :NN] = cos_y[: half * ROWS_Y].reshape(half, ROWS_Y, NN)
    cos_rows[0, ROWS_Y, :NN] = cos_y[half * ROWS_Y]
    sin_rows[:, :ROWS_Y, 96 : 96 + NN] = sin_y[: half * ROWS_Y].reshape(half, ROWS_Y, NN)
    return (
        cos_rows.reshape(half * 32, 768).astype(BF16),
        sin_rows.reshape(half * 32, 896).astype(BF16),
    )


def iota(shape, dim):
    return lax.broadcasted_iota(jnp.int32, shape, dim)


def onehot(mask):
    return jnp.where(mask, 1.0, 0.0).astype(BF16)


def dot(a, b, contract_b=0):
    return lax.dot_general(a, b, (((1,), (contract_b,)), ((), ())), preferred_element_type=F32)


def order_kernel(level_ref, fields_ref, out_ref):
    for r in range(N_GX):
        out_ref[r, 0:ROWS_Y, :] = fields_ref[level_ref[0, r]]
        out_ref[r, ROWS_Y:, :] = jnp.zeros((24 - ROWS_Y, LANE), BF16)


def slot_kernel(gy_ref, owner_ref, count_ref, rows_ref, own_ref):
    blocks = M // LANE
    owner = owner_ref[...]
    hot = onehot(iota((N_GY, M), 0) == owner)
    stacked = jnp.concatenate([hot[:, b * LANE : (b + 1) * LANE] for b in range(blocks)], 0)
    source = iota((LANE, 2 * LANE), 0)
    target = iota((LANE, 2 * LANE), 1)
    prefix = dot(stacked, onehot((source < target) | (target >= LANE)))
    before = jnp.zeros((N_GY, LANE), F32)
    within = []
    for b in range(blocks):
        part = prefix[b * N_GY : (b + 1) * N_GY]
        rank = part[:, :LANE] + before
        before = before + part[:, LANE:]
        picked = hot[:, b * LANE : (b + 1) * LANE].astype(F32) * rank
        within.append(jnp.sum(picked, axis=0, keepdims=True))
    within = jnp.concatenate(within, 1).astype(jnp.int32)
    low = jnp.where(within < 16, owner * 16 + within, -1)
    high = jnp.where(within >= 16, owner * 16 + within - 16, -1)
    rows_ref[...] = jnp.concatenate([low, high], 0)
    slot = owner * MCAP + within
    mine = gy_ref[0, 0] * MCAP + iota((MCAP, M), 0) == slot
    counts = jnp.sum(jnp.where(mine, count_ref[...].astype(F32), 0.0), axis=1, keepdims=True)
    own_ref[...] = jnp.broadcast_to(counts, (MCAP, LANE)).astype(jnp.int32)


def x_kernel(grid_ref, rows_ref, table_hbm, out_ref, table_ref, sems):
    chunks = 4
    size = M // chunks
    copies = [
        pltpu.make_async_copy(
            table_hbm.at[pl.ds(i * size, size)], table_ref.at[pl.ds(i * size, size)], sems.at[i]
        )
        for i in range(chunks)
    ]
    for c in copies:
        c.start()
    k = iota((2 * LANE, LANE), 0)
    i = iota((2 * LANE, LANE), 1)
    flip = onehot(((k < LANE) & (i >= 1) & (k == LANE - i)) | ((k == LANE) & (i == 0)))
    half = N_GX // 2
    pairs = [
        jnp.concatenate([grid_ref[N_GX - 1 - b], grid_ref[(N_GX - b) % N_GX]], 1)
        for b in range(half)
    ]
    mirror = dot(jnp.concatenate(pairs, 0), flip)
    lead = [grid_ref[b].astype(F32) for b in range(half)]
    even = [(lead[b] + mirror[b * 24 : (b + 1) * 24]).astype(BF16) for b in range(half)]
    odd = [(lead[b] - mirror[b * 24 : (b + 1) * 24]).astype(BF16) for b in range(half)]
    middle = grid_ref[half].astype(F32)
    even.append((middle + middle).astype(BF16))
    even = jnp.concatenate(even, 1)
    odd = jnp.concatenate(odd, 1)
    pad = jnp.zeros((8, KX), BF16)
    top = jnp.concatenate([even, jnp.zeros((24, M), BF16)], 1)
    bottom = jnp.concatenate([jnp.zeros((24, M + LANE), BF16), odd], 1)
    folded = jnp.concatenate([top, pad, bottom, pad], 0)
    place = iota((M, M), 0)
    low = onehot(place == rows_ref[0:1, :])
    high = onehot(iota((M // 1, M), 0) == rows_ref[1:2, :])
    spectra = []
    for j in range(chunks):
        copies[j].wait()
        part = table_ref[j * size : (j + 1) * size, :]
        spectra.append(dot(part, folded, 1).astype(BF16))
    spectra = jnp.concatenate(spectra, 0)
    none = jnp.zeros((M, 64), BF16)
    first = jnp.concatenate([spectra, none], 1)
    second = jnp.concatenate([none, spectra], 1)
    placed = dot(low, first) + dot(high, second)
    out_ref[...] = placed.astype(BF16).reshape(N_GY, 16, LANE)


def y_kernel(got_ref, own_ref, cos_hbm, sin_hbm, out_ref, cos_ref, sin_ref, sems):
    copies = [
        pltpu.make_async_copy(cos_hbm, cos_ref, sems.at[0]),
        pltpu.make_async_copy(sin_hbm, sin_ref, sems.at[1]),
    ]
    for c in copies:
        c.start()
    half = N_GY // 2
    groups = half // 4
    n = iota((1, 512), 1)
    wanted_g = n // 128
    wanted_u = (n // 32) % 4
    j = n % 32
    lead_key = jnp.where(j < ROWS_Y, wanted_u * 128 + wanted_g * 32 + j, -1)
    lead_perm = onehot(iota((512, 512), 0) == lead_key)
    mirror_key = jnp.where(
        j == 0,
        (4 - wanted_u) * 128 + wanted_g * 32,
        jnp.where(j < ROWS_Y, (3 - wanted_u) * 128 + wanted_g * 32 + ROWS_Y - j, -1),
    )
    mirror_perm = onehot(iota((640, 512), 0) == mirror_key)
    middle_key = jnp.where((j == ROWS_Y) & (wanted_u == 0), wanted_g * 32, -1)
    middle_perm = onehot(iota((128, 512), 0) == middle_key)
    lead = jnp.concatenate(
        [jnp.concatenate([got_ref[4 * t + u] for u in range(4)], 1) for t in range(groups)], 0
    )
    back = jnp.concatenate(
        [
            jnp.concatenate([got_ref[(60 - 4 * t + v) % N_GY] for v in range(5)], 1)
            for t in range(groups)
        ],
        0,
    )
    lead = dot(lead, lead_perm)
    mirror = dot(back, mirror_perm)
    middle = dot(got_ref[half], middle_perm)
    even = lead + mirror
    odd = (lead - mirror).astype(BF16)
    even = jnp.concatenate([even[:16] + 2.0 * middle, even[16:]], 0).astype(BF16)

    def rows_of(v):
        return jnp.concatenate(
            [
                jnp.concatenate(
                    [v[t * 16 : (t + 1) * 16, g * LANE : (g + 1) * LANE] for t in range(groups)], 1
                )
                for g in range(4)
            ],
            0,
        )

    even = rows_of(even)
    odd = rows_of(odd)
    copies[0].wait()
    cos_part = dot(even, cos_ref[...])
    copies[1].wait()
    sin_part = dot(odd, sin_ref[...])
    both = jnp.concatenate(
        [cos_part[:, :640], cos_part[:, 640:] + sin_part[:, :LANE], sin_part[:, LANE:]], 1
    )[:, : 2 * NN]
    lane = iota((MCAP, 2 * NN), 1)
    lane = jnp.where(lane >= NN, lane - NN, lane)
    keep = lane < own_ref[:, 0:1]
    parts = []
    for c in range(2):
        part = jnp.concatenate([both[c * 16 : c * 16 + 16], both[32 + c * 16 : 40 + c * 16]], 0)
        parts.append(jnp.where(keep, part, 0.0))
    out_ref[0] = jnp.concatenate(parts, 1)


def vmem():
    return pl.BlockSpec(memory_space=pltpu.VMEM)


def smem():
    return pl.BlockSpec(memory_space=pltpu.SMEM)


def hbm():
    return pl.BlockSpec(memory_space=pl.ANY)


def order_levels(level_order, fields):
    return pl.pallas_call(
        order_kernel,
        out_shape=jax.ShapeDtypeStruct((N_GX, 24, LANE), BF16),
        in_specs=[smem(), vmem()],
        out_specs=vmem(),
        name="order_levels",
    )(level_order.reshape(1, N_GX), fields)


def find_slots(gy, m_owner, n_count):
    return pl.pallas_call(
        slot_kernel,
        out_shape=(
            jax.ShapeDtypeStruct((2, M), jnp.int32),
            jax.ShapeDtypeStruct((MCAP, LANE), jnp.int32),
        ),
        in_specs=[smem(), vmem(), vmem()],
        out_specs=(vmem(), vmem()),
        cost_estimate=pl.CostEstimate(flops=200_000_000, bytes_accessed=100_000, transcendentals=0),
        name="slots",
    )(gy.reshape(1, 1), m_owner.reshape(1, M), n_count.reshape(1, M))


def x_transform(grid, rows, table):
    return pl.pallas_call(
        x_kernel,
        out_shape=jax.ShapeDtypeStruct((N_GY, 16, LANE), BF16),
        in_specs=[vmem(), vmem(), hbm()],
        out_specs=vmem(),
        scratch_shapes=[pltpu.VMEM((M, KX), BF16), pltpu.SemaphoreType.DMA((4,))],
        name="x_transform",
    )(grid, rows, table)


def y_transform(arrived, own, cos_y, sin_y):
    return pl.pallas_call(
        y_kernel,
        out_shape=jax.ShapeDtypeStruct((1, MCAP, 4 * NN), F32),
        in_specs=[vmem(), vmem(), hbm(), hbm()],
        out_specs=vmem(),
        scratch_shapes=[
            pltpu.VMEM((1024, 768), BF16),
            pltpu.VMEM((1024, 896), BF16),
            pltpu.SemaphoreType.DMA((2,)),
        ],
        name="y_transform",
    )(arrived, own, cos_y, sin_y)


def body(fields, level_order, m_owner, n_count):
    table_x = jnp.asarray(x_table())
    cos_y, sin_y = (jnp.asarray(t) for t in y_tables())
    ordered = order_levels(level_order, fields)
    grid = lax.all_to_all(ordered, "gx", split_axis=0, concat_axis=0, tiled=True)
    rows, own = find_slots(lax.axis_index("gy"), m_owner, n_count)
    outgoing = x_transform(grid, rows, table_x)
    arrived = lax.all_to_all(outgoing, "gy", split_axis=0, concat_axis=0, tiled=True)
    return y_transform(arrived, own, cos_y, sin_y)


def solution(mesh):
    in_specs = (P(None, "gy", "gx"), P(), P(), P())
    out_specs = P("gx", "gy", None)
    return jax.shard_map(body, mesh=mesh, in_specs=in_specs, out_specs=out_specs, check_vma=False)
```

profile of v0, /device:TPU:1, one launch (start us, length us, event | category | flops | bytes accessed | tf_op | source)
XLA Modules:
  0.0 72.1 jit_solution(13398112735849294624)
XLA Ops:
  0.0 1.6 %copy.8.fields_ref = bf16[16,23,128]{2,1,0:T(8,128)(2,1)} copy(bf16[16,23,128]{2,0,1:T(8,128)(2,1)} %param.7) | data formatting | bytes 188416 | tf_op args[0]
  1.6 1.6 %order_levels.1 = bf16[16,24,128]{2,1,0:T(8,128)(2,1)} custom-call(s32[1,16]{1,0:T(1,128)} %bitcast.4, bf16[16,23,128]{2,1,0:T(8,128)(2,1)} %copy.8.fields_ref), custom_call_target="tpu_custom_call" | custom-call | tf_op jit(solution)/shard_map/order_levels/pallas_call | solution.py:235
  3.1 19.4 %all-to-all-start = ((bf16[16,24,128]{2,1,0:T(8,128)(2,1)}), bf16[16,24,128]{2,1,0:T(8,128)(2,1)S(1)}, u32[]{:S(2)}, u32[]{:S(2)}) async-start(bf16[16,24,128]{2,1,0:T(8,128)(2,1)} %order_levels.1), calls=%async_computation | async-start | bytes 196608 | tf_op jit(solution)/shard_map/all_to_all | solution.py:288
  22.5 1.6 %slots.1 = (s32[2,1024]{1,0:T(2,128)}, s32[24,128]{1,0:T(8,128)}) custom-call(s32[1,1]{1,0:T(1,128)} %bitcast.1.gy_ref, s32[1,1024]{1,0:T(1,128)} %bitcast.5, s32[1,1024]{1,0:T(1,128)} %bitcast.6), custom_call_target="tpu_custom_call" | custom-call | flops 200000000 | bytes 100000 | tf_op jit(solution)/shard_map/slots/pallas_call | solution.py:245
  24.2 10.2 %all-to-all-done.grid_ref = bf16[16,24,128]{2,1,0:T(8,128)(2,1)S(1)} async-done(((bf16[16,24,128]{2,1,0:T(8,128)(2,1)}), bf16[16,24,128]{2,1,0:T(8,128)(2,1)S(1)}, u32[]{:S(2)}, u32[]{:S(2)}) %all-to-all-start) | async-done | bytes 98336 | tf_op jit(solution)/shard_map/all_to_all | solution.py:288
  34.4 0.0 copy-start
  34.4 0.6 copy-done
  35.0 6.8 %x_transform.1 = bf16[64,16,128]{2,1,0:T(8,128)(2,1)} custom-call(bf16[16,24,128]{2,1,0:T(8,128)(2,1)} %copy-done, s32[2,1024]{1,0:T(2,128)} %get-tuple-element.7.rows_ref, bf16[1024,2176]{1,0:T(8,128)(2,1)} %constant.12.clone.table_hbm), custom_call_target="tpu_custom_call" | custom-call | tf_op jit(solution)/shard_map/x_transform/pallas_call | solution.py:259
  41.9 26.1 %all_to_all.10.got_ref = bf16[64,16,128]{2,1,0:T(8,128)(2,1)} all-to-all(bf16[64,16,128]{2,1,0:T(8,128)(2,1)} %x_transform.1), channel_id=1, replica_groups=mesh['gy'=64,'gx'=16] {'gy'}, dimensions={0} | all-to-all | bytes 524288 | tf_op jit(solution)/shard_map/all_to_all | solution.py:291
  67.9 4.2 %y_transform.1 = f32[1,24,2944]{2,1,0:T(8,128)} custom-call(bf16[64,16,128]{2,1,0:T(8,128)(2,1)} %all_to_all.10.got_ref, s32[24,128]{1,0:T(8,128)} %get-tuple-element.8.own_ref, bf16[1024,768]{1,0:T(8,128)(2,1)} %constant.13.clone.cos_hbm, bf16[1024,896]{1,0:T(8,128)(2,1)} %constant.14.clone.sin_hbm), custom_call_target="tpu_custom_call" | custom-call | tf_op jit(solution)/shard_map/y_transform/pallas_call | solution.py:270
Async XLA Ops:
  3.1 31.3 %all-to-all-start = ((bf16[16,24,128]{2,1,0:T(8,128)(2,1)}), bf16[16,24,128]{2,1,0:T(8,128)(2,1)S(1)}, u32[]{:S(2)}, u32[]{:S(2)}) async-start(bf16[16,24,128]{2,1,0:T(8,128)(2,1)} %order_levels.1), calls=%async_computation | async-start | bytes 196608 | tf_op jit(solution)/shard_map/all_to_all | solution.py:288
  34.4 0.6 copy-start
where the time goes:
time: 72.5 us; the launch traced here: 72.1 us
  blocking collectives  26.1 us (36%)
  starting transfers between devices  19.4 us (27%)
  Pallas kernels  14.3 us (20%)
  waiting for transfers between devices  10.2 us (14%)
  local copies, waits for them, and re-layouts  2.18 us (3%)
    all_to_all x1, blocking collectives, body(): lax.all_to_all(outgoing, 'gy', split_axis=0, concat_axis=0, tiled=True)  26.1 us
    all_to_all x1, starting transfers between devices, body(): lax.all_to_all(ordered, 'gx', split_axis=0, concat_axis=0, tiled=True)  19.4 us
    all_to_all x1, waiting for transfers between devices, body(): lax.all_to_all(ordered, 'gx', split_axis=0, concat_axis=0, tiled=True)  10.2 us
    pallas_call x1, Pallas kernels, x_transform(): pl.pallas_call(x_kernel, out_shape=jax.ShapeDtypeStruct((N_GY, 16, LANE),...  6.84 us
    pallas_call x1, Pallas kernels, y_transform(): pl.pallas_call(y_kernel, out_shape=jax.ShapeDtypeStruct((1, MCAP, 4 * NN)...  4.22 us
    unnamed x3, local copies, waits for them, and re-layouts  2.18 us
    pallas_call x1, Pallas kernels, find_slots(): pl.pallas_call(slot_kernel, out_shape=(jax.ShapeDtypeStruct((2, M), jnp.i...  1.63 us
    pallas_call x1, Pallas kernels, order_levels(): pl.pallas_call(order_kernel, out_shape=jax.ShapeDtypeStruct((N_GX, 24, LA...  1.56 us
  transfers between devices with their start and end apart: 1, of which 1 were waited for; matrix products, arithmetic and copies ran while one was open for 0% of the time, Pallas kernels for 2%

commit v1 on v0

v1 whole, which is shorter than its diff:
```python
import math

import jax
import jax.numpy as jnp
import numpy as np
from jax import lax
from jax.experimental import pallas as pl
from jax.experimental.pallas import tpu as pltpu
from jax.sharding import PartitionSpec as P

NX = 2048
NY = 1472
M = 1024
NN = 736
MCAP = 24
N_GY = 64
N_GX = 16
ROWS_Y = 23
LANE = 128
VMEM_LIMIT = 32 << 20
F32 = jnp.float32
BF16 = jnp.bfloat16


def mode_tables(extent, mode_total):
    middle = extent // 2
    points = np.arange(middle + 1, dtype=np.int64)
    orders = np.arange(mode_total, dtype=np.int64)
    phases = (points[:, None] * orders[None, :] % extent).astype(np.float32) * np.float32(
        2.0 * math.pi / extent
    )
    weight = np.where((points == 0) | (points == middle), 0.5, 1.0).astype(np.float32)
    factor = np.float32(1.0 / math.sqrt(extent))
    cos_even = weight[:, None] * np.cos(phases) * factor
    sin_odd = -np.sin(phases) * factor
    return cos_even, sin_odd


def x_tables():
    cos_x, sin_x = mode_tables(NX, M)
    cos_rows = np.zeros((M + LANE, M), np.float32)
    cos_rows[: M + 1] = cos_x
    return cos_rows.astype(BF16), sin_x[:M].astype(BF16)


def y_tables():
    cos_y, sin_y = mode_tables(NY, NN)
    half = N_GY // 2
    cos_rows = np.zeros((half, 32, 768), np.float32)
    sin_rows = np.zeros((half, 32, 896), np.float32)
    cos_rows[:, :ROWS_Y, :NN] = cos_y[: half * ROWS_Y].reshape(half, ROWS_Y, NN)
    cos_rows[0, ROWS_Y, :NN] = cos_y[half * ROWS_Y]
    sin_rows[:, :ROWS_Y, 96 : 96 + NN] = sin_y[: half * ROWS_Y].reshape(half, ROWS_Y, NN)
    return (
        cos_rows.reshape(half * 32, 768).astype(BF16),
        sin_rows.reshape(half * 32, 896).astype(BF16),
    )


def iota(shape, dim):
    return lax.broadcasted_iota(jnp.int32, shape, dim)


def onehot(mask):
    return jnp.where(mask, 1.0, 0.0).astype(BF16)


def dot(a, b, contract_b=0):
    return lax.dot_general(a, b, (((1,), (contract_b,)), ((), ())), preferred_element_type=F32)


def order_kernel(
    level_hbm, fields_hbm, owner_hbm, count_hbm, out_ref, rows_ref, own_ref,
    level_ref, fields_ref, owner_ref, count_ref, sems,
):
    fetches = [
        pltpu.make_async_copy(source, target, sems.at[i])
        for i, (source, target) in enumerate(
            (
                (level_hbm, level_ref),
                (fields_hbm, fields_ref),
                (owner_hbm, owner_ref),
                (count_hbm, count_ref),
            )
        )
    ]
    for fetch in fetches:
        fetch.start()
    fetches[0].wait()
    rows = N_GX * 24
    row = iota((rows, 1), 0)
    level = jnp.zeros((rows, 1), jnp.int32)
    for r in range(N_GX):
        level = jnp.where(row >= r * 24, level_ref[0, r], level)
    y = row % 24
    key = jnp.where(y < ROWS_Y, y * N_GX + level, -1)
    pick = onehot(iota((rows, 24 * N_GX), 1) == key)
    for fetch in fetches[1:]:
        fetch.wait()
    data = fields_ref[...].reshape(ROWS_Y * N_GX, LANE)
    data = jnp.concatenate([data, jnp.zeros((N_GX, LANE), BF16)], 0)
    out_ref[...] = dot(pick, data).astype(BF16).reshape(N_GX, 24, LANE)
    find_slots(owner_ref[...], count_ref[...], rows_ref, own_ref)


def find_slots(owner, count, rows_ref, own_ref):
    blocks = M // LANE
    hot = onehot(iota((N_GY, M), 0) == owner)
    stacked = jnp.concatenate([hot[:, b * LANE : (b + 1) * LANE] for b in range(blocks)], 0)
    source = iota((LANE, 2 * LANE), 0)
    target = iota((LANE, 2 * LANE), 1)
    prefix = dot(stacked, onehot((source < target) | (target >= LANE)))
    before = jnp.zeros((N_GY, LANE), F32)
    within = []
    for b in range(blocks):
        part = prefix[b * N_GY : (b + 1) * N_GY]
        rank = part[:, :LANE] + before
        before = before + part[:, LANE:]
        picked = hot[:, b * LANE : (b + 1) * LANE].astype(F32) * rank
        within.append(jnp.sum(picked, axis=0, keepdims=True))
    within = jnp.concatenate(within, 1).astype(jnp.int32)
    low = jnp.where(within < 16, owner * 16 + within, -1)
    high = jnp.where(within >= 16, owner * 8 + within - 16, -1)
    rows_ref[...] = jnp.concatenate([low, high], 0)
    mine = lax.axis_index("gy") * MCAP + iota((MCAP, M), 0) == owner * MCAP + within
    counts = jnp.sum(jnp.where(mine, count.astype(F32), 0.0), axis=1, keepdims=True)
    own_ref[...] = jnp.broadcast_to(counts, (MCAP, LANE)).astype(jnp.int32)


def x_kernel(grid_ref, rows_ref, cos_ref, sin_ref, out_ref):
    low = onehot(iota((N_GY * 16, M), 0) == rows_ref[0:1, :])
    high = onehot(iota((N_GY * 8, M), 0) == rows_ref[1:2, :])
    k = iota((2 * LANE, LANE), 0)
    i = iota((2 * LANE, LANE), 1)
    flip = onehot(((k < LANE) & (i >= 1) & (k == LANE - i)) | ((k == LANE) & (i == 0)))
    half = N_GX // 2
    pairs = [
        jnp.concatenate([grid_ref[N_GX - 1 - b], grid_ref[(N_GX - b) % N_GX]], 1)
        for b in range(half)
    ]
    mirror = dot(jnp.concatenate(pairs, 0), flip)
    lead = [grid_ref[b].astype(F32) for b in range(half)]
    even = [(lead[b] + mirror[b * 24 : (b + 1) * 24]).astype(BF16) for b in range(half)]
    odd = [(lead[b] - mirror[b * 24 : (b + 1) * 24]).astype(BF16) for b in range(half)]
    middle = grid_ref[half].astype(F32)
    even.append((middle + middle).astype(BF16))
    across = dot(jnp.concatenate(odd, 1), sin_ref[...])
    along = dot(jnp.concatenate(even, 1), cos_ref[...])
    pad = jnp.zeros((8, M), F32)
    spectra = jnp.concatenate([along, pad, across, pad], 0).astype(BF16)
    none = jnp.zeros((64, M), BF16)
    low = dot(low, jnp.concatenate([spectra, none], 0), 1).reshape(N_GY, 16, LANE)
    high = dot(high, jnp.concatenate([none, spectra], 0), 1).reshape(N_GY, 8, LANE)
    out_ref[:, :8, :] = (low[:, :8] + high).astype(BF16)
    out_ref[:, 8:, :] = low[:, 8:].astype(BF16)


def y_kernel(got_ref, own_ref, cos_ref, sin_ref, out_ref):
    half = N_GY // 2
    groups = half // 4
    n = iota((1, 512), 1)
    wanted_g = n // 128
    wanted_u = (n // 32) % 4
    j = n % 32
    lead_key = jnp.where(j < ROWS_Y, wanted_u * 128 + wanted_g * 32 + j, -1)
    lead_perm = onehot(iota((512, 512), 0) == lead_key)
    mirror_key = jnp.where(
        j == 0,
        (4 - wanted_u) * 128 + wanted_g * 32,
        jnp.where(j < ROWS_Y, (3 - wanted_u) * 128 + wanted_g * 32 + ROWS_Y - j, -1),
    )
    mirror_perm = onehot(iota((640, 512), 0) == mirror_key)
    middle_key = jnp.where((j == ROWS_Y) & (wanted_u == 0), wanted_g * 32, -1)
    middle_perm = onehot(iota((128, 512), 0) == middle_key)
    lead = jnp.concatenate(
        [jnp.concatenate([got_ref[4 * t + u] for u in range(4)], 1) for t in range(groups)], 0
    )
    back = jnp.concatenate(
        [
            jnp.concatenate([got_ref[(60 - 4 * t + v) % N_GY] for v in range(5)], 1)
            for t in range(groups)
        ],
        0,
    )
    lead = dot(lead, lead_perm)
    mirror = dot(back, mirror_perm)
    middle = dot(got_ref[half], middle_perm)
    even = lead + mirror
    odd = (lead - mirror).astype(BF16)
    even = jnp.concatenate([even[:16] + 2.0 * middle, even[16:]], 0).astype(BF16)

    def rows_of(v):
        return jnp.concatenate(
            [
                jnp.concatenate(
                    [v[t * 16 : (t + 1) * 16, g * LANE : (g + 1) * LANE] for t in range(groups)], 1
                )
                for g in range(4)
            ],
            0,
        )

    even = rows_of(even)
    odd = rows_of(odd)
    sin_part = dot(odd, sin_ref[...])
    cos_part = dot(even, cos_ref[...])
    both = jnp.concatenate(
        [cos_part[:, :640], cos_part[:, 640:] + sin_part[:, :LANE], sin_part[:, LANE:]], 1
    )[:, : 2 * NN]
    lane = iota((MCAP, 2 * NN), 1)
    lane = jnp.where(lane >= NN, lane - NN, lane)
    keep = lane < own_ref[:, 0:1]
    parts = []
    for c in range(2):
        part = jnp.concatenate([both[c * 16 : c * 16 + 16], both[32 + c * 16 : 40 + c * 16]], 0)
        parts.append(jnp.where(keep, part, 0.0))
    out_ref[0] = jnp.concatenate(parts, 1)


def vmem():
    return pl.BlockSpec(memory_space=pltpu.VMEM)


def hbm():
    return pl.BlockSpec(memory_space=pltpu.HBM)


def held(x):
    return pltpu.with_memory_space_constraint(x, pltpu.VMEM)


def far(x):
    return pltpu.with_memory_space_constraint(x, pltpu.HBM)


def order_levels(level_order, fields, m_owner, n_count):
    args = (
        level_order.reshape(1, N_GX),
        fields.transpose(1, 0, 2),
        m_owner.reshape(1, M),
        n_count.reshape(1, M),
    )
    return pl.pallas_call(
        order_kernel,
        out_shape=(
            pltpu.VMEM((N_GX, 24, LANE), BF16),
            pltpu.VMEM((2, M), jnp.int32),
            pltpu.VMEM((MCAP, LANE), jnp.int32),
        ),
        in_specs=[hbm()] * 4,
        out_specs=(vmem(),) * 3,
        scratch_shapes=[
            pltpu.SMEM((1, N_GX), jnp.int32),
            pltpu.VMEM(args[1].shape, BF16),
            pltpu.VMEM((1, M), jnp.int32),
            pltpu.VMEM((1, M), jnp.int32),
            pltpu.SemaphoreType.DMA((4,)),
        ],
        name="order_levels",
        cost_estimate=pl.CostEstimate(flops=4000000000, bytes_accessed=100000, transcendentals=0),
        compiler_params=pltpu.CompilerParams(vmem_limit_bytes=VMEM_LIMIT),
    )(*(far(x) for x in args))


def x_transform(grid, rows, cos_x, sin_x):
    return pl.pallas_call(
        x_kernel,
        out_shape=pltpu.VMEM((N_GY, 16, LANE), BF16),
        in_specs=[vmem(), vmem(), vmem(), vmem()],
        out_specs=vmem(),
        name="x_transform",
        compiler_params=pltpu.CompilerParams(vmem_limit_bytes=VMEM_LIMIT),
    )(held(grid), held(rows), held(cos_x), held(sin_x))


def y_transform(arrived, own, cos_y, sin_y):
    return pl.pallas_call(
        y_kernel,
        out_shape=jax.ShapeDtypeStruct((1, MCAP, 4 * NN), F32),
        in_specs=[vmem(), vmem(), vmem(), vmem()],
        out_specs=vmem(),
        name="y_transform",
        compiler_params=pltpu.CompilerParams(vmem_limit_bytes=VMEM_LIMIT),
    )(held(arrived), held(own), held(cos_y), held(sin_y))


def body(fields, level_order, m_owner, n_count):
    cos_x, sin_x = (jnp.asarray(t) for t in x_tables())
    cos_y, sin_y = (jnp.asarray(t) for t in y_tables())
    ordered, rows, own = order_levels(level_order, fields, m_owner, n_count)
    grid = lax.all_to_all(ordered, "gx", split_axis=0, concat_axis=0, tiled=True)
    outgoing = x_transform(grid, rows, cos_x, sin_x)
    arrived = lax.all_to_all(outgoing, "gy", split_axis=0, concat_axis=0, tiled=True)
    return y_transform(arrived, own, cos_y, sin_y)


def solution(mesh):
    in_specs = (P(None, "gy", "gx"), P(), P(), P())
    out_specs = P("gx", "gy", None)
    return jax.shard_map(body, mesh=mesh, in_specs=in_specs, out_specs=out_specs, check_vma=False)
```

time: 72.5 us -> 62.2 us (0.86)
  blocking collectives: 26.1 us -> 56.8 us
  starting transfers between devices: 19.4 us -> 0 us
  waiting for transfers between devices: 10.2 us -> 0 us
  Pallas kernels: 14.3 us -> 5.21 us
  local copies, waits for them, and re-layouts: 2.18 us -> 0.01 us
    all_to_all x0 -> x1, blocking collectives: none -> 31.1 us  [body(): lax.all_to_all(ordered, 'gx', split_axis=0, concat_axis=0, tiled=True)]
    all_to_all x1 -> x0, starting transfers between devices: 19.4 us -> none  [body(): lax.all_to_all(ordered, 'gx', split_axis=0, concat_axis=0, tiled=True)]
    all_to_all x1 -> x0, waiting for transfers between devices: 10.2 us -> none  [body(): lax.all_to_all(ordered, 'gx', split_axis=0, concat_axis=0, tiled=True)]
    pallas_call x3 -> x2, Pallas kernels: 10 us -> 3.36 us  [the longest x1 1.87 us: x_transform(): pl.pallas_call(x_kernel, out_shape=pltpu.VMEM((N_GY, 16, LANE), BF16), in...]
    pallas_call x1, Pallas kernels: 4.22 us -> 1.86 us  [y_transform(): pl.pallas_call(y_kernel, out_shape=jax.ShapeDtypeStruct((1, MCAP, 4 * NN)...]
    unnamed x3 -> x8, local copies, waits for them, and re-layouts: 2.18 us -> 0.01 us
  transfers between devices with their start and end apart: 1 -> 0, of which waited for: 1 -> 0; matrix products, arithmetic and copies ran while one was open for 0% -> 0% of each run, Pallas kernels for 2% -> 0%
where the time goes in v1:
time: 62.2 us; the launch traced here: 62.1 us
  blocking collectives  56.8 us (91%)
  Pallas kernels  5.21 us (8%)
    all_to_all x1, blocking collectives, body(): lax.all_to_all(ordered, 'gx', split_axis=0, concat_axis=0, tiled=True)  31.1 us
    all_to_all x1, blocking collectives, body(): lax.all_to_all(outgoing, 'gy', split_axis=0, concat_axis=0, tiled=True)  25.7 us
    pallas_call x1, Pallas kernels, x_transform(): pl.pallas_call(x_kernel, out_shape=pltpu.VMEM((N_GY, 16, LANE), BF16), in...  1.87 us
    pallas_call x1, Pallas kernels, y_transform(): pl.pallas_call(y_kernel, out_shape=jax.ShapeDtypeStruct((1, MCAP, 4 * NN)...  1.86 us
    pallas_call x1, Pallas kernels, order_levels(): pl.pallas_call(order_kernel, out_shape=(pltpu.VMEM((N_GX, 24, LANE), BF16...  1.48 us

profile of v1, /device:TPU:1, one launch (start us, length us, event | category | flops | bytes accessed | tf_op | source)
XLA Modules:
  0.0 62.1 jit_solution(6516379171170426767)
XLA Ops:
  0.0 0.0 copy-start
  0.0 0.0 copy-start.1
  0.0 1.5 %order_levels.1 = (bf16[16,24,128]{2,1,0:T(8,128)(2,1)S(1)}, s32[2,1024]{1,0:T(2,128)S(1)}, s32[24,128]{1,0:T(8,128)S(1)}) custom-call(s32[1,16]{1,0:T(1,128)} %bitcast.7, bf16[23,16,128]{2,1,0:T(8,128)(2,1)} %bitcast.4, s32[1,1024]{1,0:T(1,128)} %bitcast.5, s32[1,1024]{1,0:T(1,128)} %bitcast.6), custom_call_target="tpu_custom_call" | custom-call | flops 4000000000 | bytes 100000 | tf_op jit(solution)/shard_map/order_levels/pallas_call | solution.py:243
  1.5 31.1 %all_to_all.10.grid_ref = bf16[16,24,128]{2,1,0:T(8,128)(2,1)S(1)} all-to-all(bf16[16,24,128]{2,1,0:T(8,128)(2,1)S(1)} %get-tuple-element.8), channel_id=1, replica_groups=mesh['gy'=64,'gx'=16] {'gx'}, dimensions={0} | all-to-all | bytes 196608 | tf_op jit(solution)/shard_map/all_to_all | solution.py:291
  32.6 0.0 copy-done
  32.6 0.0 copy-done.1
  32.6 0.0 copy-start.2
  32.6 0.0 copy-start.3
  32.6 1.9 %x_transform.1 = bf16[64,16,128]{2,1,0:T(8,128)(2,1)S(1)} custom-call(bf16[16,24,128]{2,1,0:T(8,128)(2,1)S(1)} %all_to_all.10.grid_ref, s32[2,1024]{1,0:T(2,128)S(1)} %get-tuple-element.9.rows_ref, bf16[1152,1024]{1,0:T(8,128)(2,1)S(1)} %copy-done, bf16[1024,1024]{1,0:T(8,128)(2,1)S(1)} %copy-done.1), custom_call_target="tpu_custom_call" | custom-call | tf_op jit(solution)/shard_map/x_transform/pallas_call | solution.py:266
  34.4 25.7 %all_to_all.11.got_ref = bf16[64,16,128]{2,1,0:T(8,128)(2,1)S(1)} all-to-all(bf16[64,16,128]{2,1,0:T(8,128)(2,1)S(1)} %x_transform.1), channel_id=1, replica_groups=mesh['gy'=64,'gx'=16] {'gy'}, dimensions={0} | all-to-all | bytes 524288 | tf_op jit(solution)/shard_map/all_to_all | solution.py:293
  60.2 0.0 copy-done.2
  60.2 0.0 copy-done.3
  60.2 1.9 %y_transform.1 = f32[1,24,2944]{2,1,0:T(8,128)} custom-call(bf16[64,16,128]{2,1,0:T(8,128)(2,1)S(1)} %all_to_all.11.got_ref, s32[24,128]{1,0:T(8,128)S(1)} %get-tuple-element.10.own_ref, bf16[1024,768]{1,0:T(8,128)(2,1)S(1)} %copy-done.3, bf16[1024,896]{1,0:T(8,128)(2,1)S(1)} %copy-done.2), custom_call_target="tpu_custom_call" | custom-call | tf_op jit(solution)/shard_map/y_transform/pallas_call | solution.py:277
Async XLA Ops:
  0.0 32.6 %copy-start = (bf16[1152,1024]{1,0:T(8,128)(2,1)S(1)}, bf16[1152,1024]{1,0:T(8,128)(2,1)}, u32[]{:S(2)}) copy-start(bf16[1152,1024]{1,0:T(8,128)(2,1)} %constant.8.clone.cos_ref) | copy-start | bytes 7077892
  0.0 32.6 %copy-start.1 = (bf16[1024,1024]{1,0:T(8,128)(2,1)S(1)}, bf16[1024,1024]{1,0:T(8,128)(2,1)}, u32[]{:S(2)}) copy-start(bf16[1024,1024]{1,0:T(8,128)(2,1)} %constant.9.clone.sin_ref) | copy-start | bytes 6291460
  32.6 27.6 %copy-start.2 = (bf16[1024,896]{1,0:T(8,128)(2,1)S(1)}, bf16[1024,896]{1,0:T(8,128)(2,1)}, u32[]{:S(2)}) copy-start(bf16[1024,896]{1,0:T(8,128)(2,1)} %constant.11.clone.sin_ref) | copy-start | bytes 5505028
  32.6 27.6 %copy-start.3 = (bf16[1024,768]{1,0:T(8,128)(2,1)S(1)}, bf16[1024,768]{1,0:T(8,128)(2,1)}, u32[]{:S(2)}) copy-start(bf16[1024,768]{1,0:T(8,128)(2,1)} %constant.10.clone.cos_ref) | copy-start | bytes 4718596

commit v2 on v1

--- a/solution.py
+++ b/solution.py
@@ -13,6 +13,7 @@
 M = 1024
 NN = 736
 MCAP = 24
+HALF = MCAP // 2
 N_GY = 64
 N_GX = 16
 ROWS_Y = 23
@@ -55,6 +56,31 @@
         cos_rows.reshape(half * 32, 768).astype(BF16),
         sin_rows.reshape(half * 32, 896).astype(BF16),
     )
+
+
+def x_flip():
+    flip = np.zeros((2 * LANE, LANE), np.float32)
+    for i in range(1, LANE):
+        flip[LANE - i, i] = 1.0
+    flip[LANE, 0] = 1.0
+    return flip.astype(BF16)
+
+
+def y_selections():
+    lead = np.zeros((4 * LANE, 4 * LANE), np.float32)
+    mirror = np.zeros((5 * LANE, 4 * LANE), np.float32)
+    middle = np.zeros((LANE, 4 * LANE), np.float32)
+    for g in range(4):
+        middle[32 * g, LANE * g + ROWS_Y] = 1.0
+        for u in range(4):
+            for j in range(ROWS_Y):
+                n = LANE * g + 32 * u + j
+                lead[LANE * u + 32 * g + j, n] = 1.0
+                if j:
+                    mirror[LANE * (3 - u) + 32 * g + ROWS_Y - j, n] = 1.0
+                else:
+                    mirror[LANE * (4 - u) + 32 * g, n] = 1.0
+    return lead.astype(BF16), mirror.astype(BF16), middle.astype(BF16)
 
 
 def iota(shape, dim):
@@ -86,30 +112,29 @@
     ]
     for fetch in fetches:
         fetch.start()
+    source = iota((LANE, 2 * LANE), 0)
+    target = iota((LANE, 2 * LANE), 1)
+    earlier = onehot((source < target) | (target >= LANE))
     fetches[0].wait()
     rows = N_GX * 24
-    row = iota((rows, 1), 0)
-    level = jnp.zeros((rows, 1), jnp.int32)
-    for r in range(N_GX):
-        level = jnp.where(row >= r * 24, level_ref[0, r], level)
-    y = row % 24
-    key = jnp.where(y < ROWS_Y, y * N_GX + level, -1)
-    pick = onehot(iota((rows, 24 * N_GX), 1) == key)
+    lane = iota((24, rows), 1)
+    y = iota((24, rows), 0)
+    lane = jnp.where(y < ROWS_Y, lane - y * N_GX, -1)
+    pick = [jnp.where(lane == level_ref[0, r], 1.0, 0.0) for r in range(N_GX)]
+    pick = jnp.concatenate(pick, 0).astype(BF16)
     for fetch in fetches[1:]:
         fetch.wait()
     data = fields_ref[...].reshape(ROWS_Y * N_GX, LANE)
     data = jnp.concatenate([data, jnp.zeros((N_GX, LANE), BF16)], 0)
     out_ref[...] = dot(pick, data).astype(BF16).reshape(N_GX, 24, LANE)
-    find_slots(owner_ref[...], count_ref[...], rows_ref, own_ref)
-
-
-def find_slots(owner, count, rows_ref, own_ref):
+    find_slots(owner_ref[...], count_ref[...], earlier, rows_ref, own_ref)
+
+
+def find_slots(owner, count, earlier, rows_ref, own_ref):
     blocks = M // LANE
     hot = onehot(iota((N_GY, M), 0) == owner)
     stacked = jnp.concatenate([hot[:, b * LANE : (b + 1) * LANE] for b in range(blocks)], 0)
-    source = iota((LANE, 2 * LANE), 0)
-    target = iota((LANE, 2 * LANE), 1)
-    prefix = dot(stacked, onehot((source < target) | (target >= LANE)))
+    prefix = dot(stacked, earlier)
     before = jnp.zeros((N_GY, LANE), F32)
     within = []
     for b in range(blocks):
@@ -119,26 +144,34 @@
         picked = hot[:, b * LANE : (b + 1) * LANE].astype(F32) * rank
         within.append(jnp.sum(picked, axis=0, keepdims=True))
     within = jnp.concatenate(within, 1).astype(jnp.int32)
-    low = jnp.where(within < 16, owner * 16 + within, -1)
-    high = jnp.where(within >= 16, owner * 8 + within - 16, -1)
+    low = jnp.where(within < HALF, owner * HALF + within, -1)
+    high = jnp.where(within >= HALF, owner * HALF + within - HALF, -1)
     rows_ref[...] = jnp.concatenate([low, high], 0)
     mine = lax.axis_index("gy") * MCAP + iota((MCAP, M), 0) == owner * MCAP + within
     counts = jnp.sum(jnp.where(mine, count.astype(F32), 0.0), axis=1, keepdims=True)
     own_ref[...] = jnp.broadcast_to(counts, (MCAP, LANE)).astype(jnp.int32)
 
 
-def x_kernel(grid_ref, rows_ref, cos_ref, sin_ref, out_ref):
-    low = onehot(iota((N_GY * 16, M), 0) == rows_ref[0:1, :])
-    high = onehot(iota((N_GY * 8, M), 0) == rows_ref[1:2, :])
-    k = iota((2 * LANE, LANE), 0)
-    i = iota((2 * LANE, LANE), 1)
-    flip = onehot(((k < LANE) & (i >= 1) & (k == LANE - i)) | ((k == LANE) & (i == 0)))
+def slot_rows(keys):
+    row = iota((256, LANE), 0).astype(F32).astype(BF16)
+    row = jnp.concatenate([row] * (M // LANE), 1)
+    blocks = []
+    for b in range(N_GY * HALF // 256):
+        key = keys - 256 * b
+        key = jnp.where((key >= 0) & (key < 256), key, -1).astype(F32).astype(BF16)
+        blocks.append(jnp.where(row == key, jnp.ones((), BF16), jnp.zeros((), BF16)))
+    return jnp.concatenate(blocks, 0)
+
+
+def x_kernel(grid_ref, rows_ref, cos_ref, sin_ref, flip_ref, out_ref):
+    low = slot_rows(rows_ref[0:1, :])
+    high = slot_rows(rows_ref[1:2, :])
     half = N_GX // 2
     pairs = [
         jnp.concatenate([grid_ref[N_GX - 1 - b], grid_ref[(N_GX - b) % N_GX]], 1)
         for b in range(half)
     ]
-    mirror = dot(jnp.concatenate(pairs, 0), flip)
+    mirror = dot(jnp.concatenate(pairs, 0), flip_ref[...])
     lead = [grid_ref[b].astype(F32) for b in range(half)]
     even = [(lead[b] + mirror[b * 24 : (b + 1) * 24]).astype(BF16) for b in range(half)]
     odd = [(lead[b] - mirror[b * 24 : (b + 1) * 24]).astype(BF16) for b in range(half)]
@@ -149,42 +182,32 @@
     pad = jnp.zeros((8, M), F32)
     spectra = jnp.concatenate([along, pad, across, pad], 0).astype(BF16)
     none = jnp.zeros((64, M), BF16)
-    low = dot(low, jnp.concatenate([spectra, none], 0), 1).reshape(N_GY, 16, LANE)
-    high = dot(high, jnp.concatenate([none, spectra], 0), 1).reshape(N_GY, 8, LANE)
-    out_ref[:, :8, :] = (low[:, :8] + high).astype(BF16)
-    out_ref[:, 8:, :] = low[:, 8:].astype(BF16)
-
-
-def y_kernel(got_ref, own_ref, cos_ref, sin_ref, out_ref):
+    placed = dot(low, jnp.concatenate([spectra, none], 0), 1)
+    placed = placed + dot(high, jnp.concatenate([none, spectra], 0), 1)
+    out_ref[...] = placed.astype(BF16)
+
+
+def y_kernel(
+    got_ref, own_ref, cos_ref, sin_ref, lead_ref, mirror_ref, middle_ref, out_ref, wide_ref
+):
     half = N_GY // 2
     groups = half // 4
-    n = iota((1, 512), 1)
-    wanted_g = n // 128
-    wanted_u = (n // 32) % 4
-    j = n % 32
-    lead_key = jnp.where(j < ROWS_Y, wanted_u * 128 + wanted_g * 32 + j, -1)
-    lead_perm = onehot(iota((512, 512), 0) == lead_key)
-    mirror_key = jnp.where(
-        j == 0,
-        (4 - wanted_u) * 128 + wanted_g * 32,
-        jnp.where(j < ROWS_Y, (3 - wanted_u) * 128 + wanted_g * 32 + ROWS_Y - j, -1),
-    )
-    mirror_perm = onehot(iota((640, 512), 0) == mirror_key)
-    middle_key = jnp.where((j == ROWS_Y) & (wanted_u == 0), wanted_g * 32, -1)
-    middle_perm = onehot(iota((128, 512), 0) == middle_key)
+    wide_ref[: N_GY * HALF, :] = got_ref[...]
+    wide_ref[N_GY * HALF :, :] = jnp.zeros((16, LANE), BF16)
+    got = [wide_ref[HALF * s : HALF * s + 16, :] for s in range(N_GY)]
     lead = jnp.concatenate(
-        [jnp.concatenate([got_ref[4 * t + u] for u in range(4)], 1) for t in range(groups)], 0
+        [jnp.concatenate([got[4 * t + u] for u in range(4)], 1) for t in range(groups)], 0
     )
     back = jnp.concatenate(
         [
-            jnp.concatenate([got_ref[(60 - 4 * t + v) % N_GY] for v in range(5)], 1)
+            jnp.concatenate([got[(60 - 4 * t + v) % N_GY] for v in range(5)], 1)
             for t in range(groups)
         ],
         0,
     )
-    lead = dot(lead, lead_perm)
-    mirror = dot(back, mirror_perm)
-    middle = dot(got_ref[half], middle_perm)
+    lead = dot(lead, lead_ref[...])
+    mirror = dot(back, mirror_ref[...])
+    middle = dot(got[half], middle_ref[...])
     even = lead + mirror
     odd = (lead - mirror).astype(BF16)
     even = jnp.concatenate([even[:16] + 2.0 * middle, even[16:]], 0).astype(BF16)
@@ -212,7 +235,9 @@
     keep = lane < own_ref[:, 0:1]
     parts = []
     for c in range(2):
-        part = jnp.concatenate([both[c * 16 : c * 16 + 16], both[32 + c * 16 : 40 + c * 16]], 0)
+        part = jnp.concatenate(
+            [both[c * 16 : c * 16 + HALF], both[32 + c * 16 : 32 + c * 16 + HALF]], 0
+        )
         parts.append(jnp.where(keep, part, 0.0))
     out_ref[0] = jnp.concatenate(parts, 1)
 
@@ -263,25 +288,28 @@
 
 
 def x_transform(grid, rows, cos_x, sin_x):
+    args = (grid, rows, cos_x, sin_x, jnp.asarray(x_flip()))
     return pl.pallas_call(
         x_kernel,
-        out_shape=pltpu.VMEM((N_GY, 16, LANE), BF16),
-        in_specs=[vmem(), vmem(), vmem(), vmem()],
+        out_shape=pltpu.VMEM((N_GY * HALF, LANE), BF16),
+        in_specs=[vmem() for _ in args],
         out_specs=vmem(),
         name="x_transform",
         compiler_params=pltpu.CompilerParams(vmem_limit_bytes=VMEM_LIMIT),
-    )(held(grid), held(rows), held(cos_x), held(sin_x))
+    )(*(held(x) for x in args))
 
 
 def y_transform(arrived, own, cos_y, sin_y):
+    args = (arrived, own, cos_y, sin_y, *(jnp.asarray(t) for t in y_selections()))
     return pl.pallas_call(
         y_kernel,
         out_shape=jax.ShapeDtypeStruct((1, MCAP, 4 * NN), F32),
-        in_specs=[vmem(), vmem(), vmem(), vmem()],
+        in_specs=[vmem() for _ in args],
         out_specs=vmem(),
+        scratch_shapes=[pltpu.VMEM((N_GY * HALF + 16, LANE), BF16)],
         name="y_transform",
         compiler_params=pltpu.CompilerParams(vmem_limit_bytes=VMEM_LIMIT),
-    )(held(arrived), held(own), held(cos_y), held(sin_y))
+    )(*(held(x) for x in args))
 
 
 def body(fields, level_order, m_owner, n_count):
@@ -290,7 +318,9 @@
     ordered, rows, own = order_levels(level_order, fields, m_owner, n_count)
     grid = lax.all_to_all(ordered, "gx", split_axis=0, concat_axis=0, tiled=True)
     outgoing = x_transform(grid, rows, cos_x, sin_x)
+    outgoing = outgoing.reshape(N_GY * HALF // 4, 4, LANE)
     arrived = lax.all_to_all(outgoing, "gy", split_axis=0, concat_axis=0, tiled=True)
+    arrived = arrived.reshape(N_GY * HALF, LANE)
     return y_transform(arrived, own, cos_y, sin_y)
 
 

time: 62.2 us -> 61.4 us (0.987)
  blocking collectives: 56.8 us -> 55.7 us
    all_to_all x1, blocking collectives: 25.7 us -> 24.7 us  [body(): lax.all_to_all(outgoing, 'gy', split_axis=0, concat_axis=0, tiled=True)]
where the time goes in v2:
time: 61.4 us; the launch traced here: 61.2 us
  blocking collectives  55.7 us (91%)
  Pallas kernels  5.33 us (9%)
    all_to_all x1, blocking collectives, body(): lax.all_to_all(ordered, 'gx', split_axis=0, concat_axis=0, tiled=True)  31.1 us
    all_to_all x1, blocking collectives, body(): lax.all_to_all(outgoing, 'gy', split_axis=0, concat_axis=0, tiled=True)  24.7 us
    pallas_call x1, Pallas kernels, x_transform(): pl.pallas_call(x_kernel, out_shape=pltpu.VMEM((N_GY * HALF, LANE), BF16),...  1.97 us
    pallas_call x1, Pallas kernels, y_transform(): pl.pallas_call(y_kernel, out_shape=jax.ShapeDtypeStruct((1, MCAP, 4 * NN)...  1.88 us
    pallas_call x1, Pallas kernels, order_levels(): pl.pallas_call(order_kernel, out_shape=(pltpu.VMEM((N_GX, 24, LANE), BF16...  1.49 us

profile of v2, /device:TPU:1, one launch (start us, length us, event | category | flops | bytes accessed | tf_op | source)
XLA Modules:
  0.0 61.2 jit_solution(7701767768561280737)
XLA Ops:
  0.0 0.0 copy-start
  0.0 0.0 copy-start.1
  0.0 0.0 copy-start.7
  0.0 1.5 %order_levels.1 = (bf16[16,24,128]{2,1,0:T(8,128)(2,1)S(1)}, s32[2,1024]{1,0:T(2,128)S(1)}, s32[24,128]{1,0:T(8,128)S(1)}) custom-call(s32[1,16]{1,0:T(1,128)} %bitcast.11, bf16[23,16,128]{2,1,0:T(8,128)(2,1)} %bitcast.8, s32[1,1024]{1,0:T(1,128)} %bitcast.9, s32[1,1024]{1,0:T(1,128)} %bitcast.10), custom_call_target="tpu_custom_call" | custom-call | flops 4000000000 | bytes 100000 | tf_op jit(solution)/shard_map/order_levels/pallas_call | solution.py:268
  1.5 31.1 %all_to_all.10.grid_ref = bf16[16,24,128]{2,1,0:T(8,128)(2,1)S(1)} all-to-all(bf16[16,24,128]{2,1,0:T(8,128)(2,1)S(1)} %get-tuple-element.8), channel_id=1, replica_groups=mesh['gy'=64,'gx'=16] {'gx'}, dimensions={0} | all-to-all | bytes 196608 | tf_op jit(solution)/shard_map/all_to_all | solution.py:319
  32.6 0.0 copy-done
  32.6 0.0 copy-done.1
  32.6 0.0 copy-done.7
  32.6 0.0 copy-start.2
  32.6 0.0 copy-start.3
  32.6 0.0 copy-start.4
  32.6 0.0 copy-start.5
  32.6 0.0 copy-start.6
  32.6 2.0 %x_transform.1 = bf16[768,128]{1,0:T(8,128)(2,1)S(1)} custom-call(bf16[16,24,128]{2,1,0:T(8,128)(2,1)S(1)} %all_to_all.10.grid_ref, s32[2,1024]{1,0:T(2,128)S(1)} %get-tuple-element.9.rows_ref, bf16[1152,1024]{1,0:T(8,128)(2,1)S(1)} %copy-done, bf16[1024,1024]{1,0:T(8,128)(2,1)S(1)} %copy-done.1, bf16[256,128]{1,0:T(8,128)(2,1)S(1)} %copy-done.7), custom_call_target="tpu_custom_call" | custom-call | tf_op jit(solution)/shard_map/x_transform/pallas_call | solution.py:292
  34.6 24.7 %all_to_all.11 = bf16[192,4,128]{2,1,0:T(4,128)(2,1)S(1)} all-to-all(bf16[192,4,128]{2,1,0:T(4,128)(2,1)S(1)} %bitcast.7), channel_id=1, replica_groups=mesh['gy'=64,'gx'=16] {'gy'}, dimensions={0} | all-to-all | bytes 393216 | tf_op jit(solution)/shard_map/all_to_all | solution.py:322
  59.3 0.0 copy-done.2
  59.3 0.0 copy-done.3
  59.3 0.0 copy-done.4
  59.3 0.0 copy-done.5
  59.3 0.0 copy-done.6
  59.3 1.9 %y_transform.1 = f32[1,24,2944]{2,1,0:T(8,128)} custom-call(bf16[768,128]{1,0:T(8,128)(2,1)S(1)} %bitcast.6, s32[24,128]{1,0:T(8,128)S(1)} %get-tuple-element.10.own_ref, bf16[1024,768]{1,0:T(8,128)(2,1)S(1)} %copy-done.3, bf16[1024,896]{1,0:T(8,128)(2,1)S(1)} %copy-done.2, bf16[512,512]{1,0:T(8,128)(2,1)S(1)} %copy-done.5, bf16[640,512]{1,0:T(8,128)(2,1)S(1)} %copy-done.4, ...), custom_call_target="tpu_custom_call" | custom-call | tf_op jit(solution)/shard_map/y_transform/pallas_call | solution.py:304
Async XLA Ops:
  0.0 32.6 %copy-start = (bf16[1152,1024]{1,0:T(8,128)(2,1)S(1)}, bf16[1152,1024]{1,0:T(8,128)(2,1)}, u32[]{:S(2)}) copy-start(bf16[1152,1024]{1,0:T(8,128)(2,1)} %constant.16.clone.cos_ref) | copy-start | bytes 7077892
  0.0 32.6 %copy-start.1 = (bf16[1024,1024]{1,0:T(8,128)(2,1)S(1)}, bf16[1024,1024]{1,0:T(8,128)(2,1)}, u32[]{:S(2)}) copy-start(bf16[1024,1024]{1,0:T(8,128)(2,1)} %constant.17.clone.sin_ref) | copy-start | bytes 6291460
  0.0 32.6 %copy-start.7 = (bf16[256,128]{1,0:T(8,128)(2,1)S(1)}, bf16[256,128]{1,0:T(8,128)(2,1)}, u32[]{:S(2)}) copy-start(bf16[256,128]{1,0:T(8,128)(2,1)} %constant.20.clone.flip_ref) | copy-start | bytes 196612
  32.6 26.7 %copy-start.2 = (bf16[1024,896]{1,0:T(8,128)(2,1)S(1)}, bf16[1024,896]{1,0:T(8,128)(2,1)}, u32[]{:S(2)}) copy-start(bf16[1024,896]{1,0:T(8,128)(2,1)} %constant.19.clone.sin_ref) | copy-start | bytes 5505028
  32.6 26.7 %copy-start.3 = (bf16[1024,768]{1,0:T(8,128)(2,1)S(1)}, bf16[1024,768]{1,0:T(8,128)(2,1)}, u32[]{:S(2)}) copy-start(bf16[1024,768]{1,0:T(8,128)(2,1)} %constant.18.clone.cos_ref) | copy-start | bytes 4718596
  32.6 26.7 %copy-start.4 = (bf16[640,512]{1,0:T(8,128)(2,1)S(1)}, bf16[640,512]{1,0:T(8,128)(2,1)}, u32[]{:S(2)}) copy-start(bf16[640,512]{1,0:T(8,128)(2,1)} %constant.22.clone.mirror_ref) | copy-start | bytes 1966084
  32.6 26.7 %copy-start.5 = (bf16[512,512]{1,0:T(8,128)(2,1)S(1)}, bf16[512,512]{1,0:T(8,128)(2,1)}, u32[]{:S(2)}) copy-start(bf16[512,512]{1,0:T(8,128)(2,1)} %constant.21.clone.lead_ref) | copy-start | bytes 1572868
  32.6 26.7 %copy-start.6 = (bf16[128,512]{1,0:T(8,128)(2,1)S(1)}, bf16[128,512]{1,0:T(8,128)(2,1)}, u32[]{:S(2)}) copy-start(bf16[128,512]{1,0:T(8,128)(2,1)} %constant.23.clone.middle_ref) | copy-start | bytes 393220

commit v3 on v2

--- a/solution.py
+++ b/solution.py
@@ -17,6 +17,7 @@
 N_GY = 64
 N_GX = 16
 ROWS_Y = 23
+FETCH_ROWS = 4
 LANE = 128
 VMEM_LIMIT = 32 << 20
 F32 = jnp.float32
@@ -95,31 +96,20 @@
     return lax.dot_general(a, b, (((1,), (contract_b,)), ((), ())), preferred_element_type=F32)
 
 
-def order_kernel(
-    level_hbm, fields_hbm, owner_hbm, count_hbm, out_ref, rows_ref, own_ref,
-    level_ref, fields_ref, owner_ref, count_ref, sems,
-):
-    fetches = [
-        pltpu.make_async_copy(source, target, sems.at[i])
-        for i, (source, target) in enumerate(
-            (
-                (level_hbm, level_ref),
-                (fields_hbm, fields_ref),
-                (owner_hbm, owner_ref),
-                (count_hbm, count_ref),
-            )
+def order_kernel(level_hbm, fields_hbm, out_ref, level_ref, fields_ref, sems):
+    fetches = [pltpu.make_async_copy(level_hbm, level_ref, sems.at[0])]
+    for i, first in enumerate(range(0, ROWS_Y, FETCH_ROWS)):
+        part = pl.ds(first, min(FETCH_ROWS, ROWS_Y - first))
+        fetches.append(
+            pltpu.make_async_copy(fields_hbm.at[part], fields_ref.at[part], sems.at[i + 1])
         )
-    ]
     for fetch in fetches:
         fetch.start()
-    source = iota((LANE, 2 * LANE), 0)
-    target = iota((LANE, 2 * LANE), 1)
-    earlier = onehot((source < target) | (target >= LANE))
-    fetches[0].wait()
     rows = N_GX * 24
     lane = iota((24, rows), 1)
     y = iota((24, rows), 0)
     lane = jnp.where(y < ROWS_Y, lane - y * N_GX, -1)
+    fetches[0].wait()
     pick = [jnp.where(lane == level_ref[0, r], 1.0, 0.0) for r in range(N_GX)]
     pick = jnp.concatenate(pick, 0).astype(BF16)
     for fetch in fetches[1:]:
@@ -127,14 +117,15 @@
     data = fields_ref[...].reshape(ROWS_Y * N_GX, LANE)
     data = jnp.concatenate([data, jnp.zeros((N_GX, LANE), BF16)], 0)
     out_ref[...] = dot(pick, data).astype(BF16).reshape(N_GX, 24, LANE)
-    find_slots(owner_ref[...], count_ref[...], earlier, rows_ref, own_ref)
-
-
-def find_slots(owner, count, earlier, rows_ref, own_ref):
+
+
+def find_slots(owner, count, own_ref):
     blocks = M // LANE
     hot = onehot(iota((N_GY, M), 0) == owner)
     stacked = jnp.concatenate([hot[:, b * LANE : (b + 1) * LANE] for b in range(blocks)], 0)
-    prefix = dot(stacked, earlier)
+    source = iota((LANE, 2 * LANE), 0)
+    target = iota((LANE, 2 * LANE), 1)
+    prefix = dot(stacked, onehot((source < target) | (target >= LANE)))
     before = jnp.zeros((N_GY, LANE), F32)
     within = []
     for b in range(blocks):
@@ -146,10 +137,10 @@
     within = jnp.concatenate(within, 1).astype(jnp.int32)
     low = jnp.where(within < HALF, owner * HALF + within, -1)
     high = jnp.where(within >= HALF, owner * HALF + within - HALF, -1)
-    rows_ref[...] = jnp.concatenate([low, high], 0)
     mine = lax.axis_index("gy") * MCAP + iota((MCAP, M), 0) == owner * MCAP + within
     counts = jnp.sum(jnp.where(mine, count.astype(F32), 0.0), axis=1, keepdims=True)
     own_ref[...] = jnp.broadcast_to(counts, (MCAP, LANE)).astype(jnp.int32)
+    return low, high
 
 
 def slot_rows(keys):
@@ -163,9 +154,8 @@
     return jnp.concatenate(blocks, 0)
 
 
-def x_kernel(grid_ref, rows_ref, cos_ref, sin_ref, flip_ref, out_ref):
-    low = slot_rows(rows_ref[0:1, :])
-    high = slot_rows(rows_ref[1:2, :])
+def x_kernel(grid_ref, owner_ref, count_ref, cos_ref, sin_ref, flip_ref, out_ref, own_ref):
+    keys = find_slots(owner_ref[...], count_ref[...], own_ref)
     half = N_GX // 2
     pairs = [
         jnp.concatenate([grid_ref[N_GX - 1 - b], grid_ref[(N_GX - b) % N_GX]], 1)
@@ -182,13 +172,14 @@
     pad = jnp.zeros((8, M), F32)
     spectra = jnp.concatenate([along, pad, across, pad], 0).astype(BF16)
     none = jnp.zeros((64, M), BF16)
+    low, high = (slot_rows(k) for k in keys)
     placed = dot(low, jnp.concatenate([spectra, none], 0), 1)
     placed = placed + dot(high, jnp.concatenate([none, spectra], 0), 1)
     out_ref[...] = placed.astype(BF16)
 
 
 def y_kernel(
-    got_ref, own_ref, cos_ref, sin_ref, lead_ref, mirror_ref, middle_ref, out_ref, wide_ref
+    got_ref, own_ref, cos_ref, sin_ref, lead_ref, mirror_ref, middle_ref, out_hbm, wide_ref, out_ref, sems
 ):
     half = N_GY // 2
     groups = half // 4
@@ -239,7 +230,26 @@
             [both[c * 16 : c * 16 + HALF], both[32 + c * 16 : 32 + c * 16 + HALF]], 0
         )
         parts.append(jnp.where(keep, part, 0.0))
-    out_ref[0] = jnp.concatenate(parts, 1)
+    cut = 11 * LANE
+    out_ref[:, :cut] = parts[0][:, :cut]
+    stores = []
+
+    def store(lanes):
+        for r in range(0, MCAP, 8):
+            stores.append(
+                pltpu.make_async_copy(
+                    out_ref.at[pl.ds(r, 8), lanes],
+                    out_hbm.at[0, pl.ds(r, 8), lanes],
+                    sems.at[len(stores)],
+                )
+            )
+            stores[-1].start()
+
+    store(pl.ds(0, cut))
+    out_ref[:, cut:] = jnp.concatenate([parts[0][:, cut:], parts[1]], 1)
+    store(pl.ds(cut, 4 * NN - cut))
+    for copy in stores:
+        copy.wait()
 
 
 def vmem():
@@ -258,42 +268,34 @@
     return pltpu.with_memory_space_constraint(x, pltpu.HBM)
 
 
-def order_levels(level_order, fields, m_owner, n_count):
-    args = (
-        level_order.reshape(1, N_GX),
-        fields.transpose(1, 0, 2),
-        m_owner.reshape(1, M),
-        n_count.reshape(1, M),
-    )
+def order_levels(level_order, fields):
+    args = (level_order.reshape(1, N_GX), fields.transpose(1, 0, 2))
     return pl.pallas_call(
         order_kernel,
-        out_shape=(
-            pltpu.VMEM((N_GX, 24, LANE), BF16),
-            pltpu.VMEM((2, M), jnp.int32),
-            pltpu.VMEM((MCAP, LANE), jnp.int32),
-        ),
-        in_specs=[hbm()] * 4,
-        out_specs=(vmem(),) * 3,
+        out_shape=pltpu.VMEM((N_GX, 24, LANE), BF16),
+        in_specs=[hbm() for _ in args],
+        out_specs=vmem(),
         scratch_shapes=[
             pltpu.SMEM((1, N_GX), jnp.int32),
             pltpu.VMEM(args[1].shape, BF16),
-            pltpu.VMEM((1, M), jnp.int32),
-            pltpu.VMEM((1, M), jnp.int32),
-            pltpu.SemaphoreType.DMA((4,)),
+            pltpu.SemaphoreType.DMA((1 + -(-ROWS_Y // FETCH_ROWS),)),
         ],
         name="order_levels",
-        cost_estimate=pl.CostEstimate(flops=4000000000, bytes_accessed=100000, transcendentals=0),
+        cost_estimate=pl.CostEstimate(flops=4_000_000_000, bytes_accessed=100_000, transcendentals=0),
         compiler_params=pltpu.CompilerParams(vmem_limit_bytes=VMEM_LIMIT),
     )(*(far(x) for x in args))
 
 
-def x_transform(grid, rows, cos_x, sin_x):
-    args = (grid, rows, cos_x, sin_x, jnp.asarray(x_flip()))
+def x_transform(grid, m_owner, n_count, cos_x, sin_x):
+    args = (grid, m_owner.reshape(1, M), n_count.reshape(1, M), cos_x, sin_x, jnp.asarray(x_flip()))
     return pl.pallas_call(
         x_kernel,
-        out_shape=pltpu.VMEM((N_GY * HALF, LANE), BF16),
+        out_shape=(
+            pltpu.VMEM((N_GY * HALF, LANE), BF16),
+            pltpu.VMEM((MCAP, LANE), jnp.int32),
+        ),
         in_specs=[vmem() for _ in args],
-        out_specs=vmem(),
+        out_specs=(vmem(), vmem()),
         name="x_transform",
         compiler_params=pltpu.CompilerParams(vmem_limit_bytes=VMEM_LIMIT),
     )(*(held(x) for x in args))
@@ -305,8 +307,12 @@
         y_kernel,
         out_shape=jax.ShapeDtypeStruct((1, MCAP, 4 * NN), F32),
         in_specs=[vmem() for _ in args],
-        out_specs=vmem(),
-        scratch_shapes=[pltpu.VMEM((N_GY * HALF + 16, LANE), BF16)],
+        out_specs=hbm(),
+        scratch_shapes=[
+            pltpu.VMEM((N_GY * HALF + 16, LANE), BF16),
+            pltpu.VMEM((MCAP, 4 * NN), F32),
+            pltpu.SemaphoreType.DMA((6,)),
+        ],
         name="y_transform",
         compiler_params=pltpu.CompilerParams(vmem_limit_bytes=VMEM_LIMIT),
     )(*(held(x) for x in args))
@@ -315,9 +321,9 @@
 def body(fields, level_order, m_owner, n_count):
     cos_x, sin_x = (jnp.asarray(t) for t in x_tables())
     cos_y, sin_y = (jnp.asarray(t) for t in y_tables())
-    ordered, rows, own = order_levels(level_order, fields, m_owner, n_count)
+    ordered = order_levels(level_order, fields)
     grid = lax.all_to_all(ordered, "gx", split_axis=0, concat_axis=0, tiled=True)
-    outgoing = x_transform(grid, rows, cos_x, sin_x)
+    outgoing, own = x_transform(grid, m_owner, n_count, cos_x, sin_x)
     outgoing = outgoing.reshape(N_GY * HALF // 4, 4, LANE)
     arrived = lax.all_to_all(outgoing, "gy", split_axis=0, concat_axis=0, tiled=True)
     arrived = arrived.reshape(N_GY * HALF, LANE)

time: 61.4 us -> 61.2 us (level)
  no operation moved by 1% of the time
where the time goes in v3:
time: 61.2 us; the launch traced here: 61 us
  blocking collectives  55.9 us (91%)
  Pallas kernels  4.98 us (8%)
    all_to_all x1, blocking collectives, body(): lax.all_to_all(ordered, 'gx', split_axis=0, concat_axis=0, tiled=True)  31.2 us
    all_to_all x1, blocking collectives, body(): lax.all_to_all(outgoing, 'gy', split_axis=0, concat_axis=0, tiled=True)  24.7 us
    pallas_call x1, Pallas kernels, x_transform(): pl.pallas_call(x_kernel, out_shape=(pltpu.VMEM((N_GY * HALF, LANE), BF16)...  1.88 us
    pallas_call x1, Pallas kernels, y_transform(): pl.pallas_call(y_kernel, out_shape=jax.ShapeDtypeStruct((1, MCAP, 4 * NN)...  1.87 us
    pallas_call x1, Pallas kernels, order_levels(): pl.pallas_call(order_kernel, out_shape=pltpu.VMEM((N_GX, 24, LANE), BF16)...  1.23 us

profile of v3, /device:TPU:1, one launch (start us, length us, event | category | flops | bytes accessed | tf_op | source)
XLA Modules:
  0.0 61.0 jit_solution(321403158992985178)
XLA Ops:
  0.0 0.0 copy-start
  0.0 0.0 copy-start.1
  0.0 0.0 copy-start.7
  0.0 0.0 copy-start.8
  0.0 0.0 copy-start.9
  0.0 1.2 %order_levels.1 = bf16[16,24,128]{2,1,0:T(8,128)(2,1)S(1)} custom-call(s32[1,16]{1,0:T(1,128)} %bitcast.11, bf16[23,16,128]{2,1,0:T(8,128)(2,1)} %bitcast.10), custom_call_target="tpu_custom_call" | custom-call | flops 4000000000 | bytes 100000 | tf_op jit(solution)/shard_map/order_levels/pallas_call | solution.py:273
  1.3 31.2 %all_to_all.10.grid_ref = bf16[16,24,128]{2,1,0:T(8,128)(2,1)S(1)} all-to-all(bf16[16,24,128]{2,1,0:T(8,128)(2,1)S(1)} %order_levels.1), channel_id=1, replica_groups=mesh['gy'=64,'gx'=16] {'gx'}, dimensions={0} | all-to-all | bytes 196608 | tf_op jit(solution)/shard_map/all_to_all | solution.py:325
  32.5 0.0 copy-done
  32.5 0.0 copy-done.1
  32.5 0.0 copy-done.7
  32.5 0.0 copy-done.8
  32.5 0.0 copy-done.9
  32.5 0.0 copy-start.2
  32.5 0.0 copy-start.3
  32.5 0.0 copy-start.4
  32.5 0.0 copy-start.5
  32.5 0.0 copy-start.6
  32.5 1.9 %x_transform.1 = (bf16[768,128]{1,0:T(8,128)(2,1)S(1)}, s32[24,128]{1,0:T(8,128)S(1)}) custom-call(bf16[16,24,128]{2,1,0:T(8,128)(2,1)S(1)} %all_to_all.10.grid_ref, s32[1,1024]{1,0:T(1,128)S(1)} %bitcast.8, s32[1,1024]{1,0:T(1,128)S(1)} %bitcast.9, bf16[1152,1024]{1,0:T(8,128)(2,1)S(1)} %copy-done, bf16[1024,1024]{1,0:T(8,128)(2,1)S(1)} %copy-done.1, ...), custom_call_target="tpu_custom_call" | custom-call | tf_op jit(solution)/shard_map/x_transform/pallas_call | solution.py:291
  34.4 24.7 %all_to_all.11 = bf16[192,4,128]{2,1,0:T(4,128)(2,1)S(1)} all-to-all(bf16[192,4,128]{2,1,0:T(4,128)(2,1)S(1)} %bitcast.7), channel_id=1, replica_groups=mesh['gy'=64,'gx'=16] {'gy'}, dimensions={0} | all-to-all | bytes 393216 | tf_op jit(solution)/shard_map/all_to_all | solution.py:328
  59.1 0.0 copy-done.2
  59.1 0.0 copy-done.3
  59.1 0.0 copy-done.4
  59.1 0.0 copy-done.5
  59.1 0.0 copy-done.6
  59.1 1.9 %y_transform.1 = f32[1,24,2944]{2,1,0:T(8,128)} custom-call(bf16[768,128]{1,0:T(8,128)(2,1)S(1)} %bitcast.6, s32[24,128]{1,0:T(8,128)S(1)} %get-tuple-element.8.own_ref, bf16[1024,768]{1,0:T(8,128)(2,1)S(1)} %copy-done.3, bf16[1024,896]{1,0:T(8,128)(2,1)S(1)} %copy-done.2, bf16[512,512]{1,0:T(8,128)(2,1)S(1)} %copy-done.5, bf16[640,512]{1,0:T(8,128)(2,1)S(1)} %copy-done.4, ...), custom_call_target="tpu_custom_call" | custom-call | tf_op jit(solution)/shard_map/y_transform/pallas_call | solution.py:306
Async XLA Ops:
  0.0 32.5 %copy-start = (bf16[1152,1024]{1,0:T(8,128)(2,1)S(1)}, bf16[1152,1024]{1,0:T(8,128)(2,1)}, u32[]{:S(2)}) copy-start(bf16[1152,1024]{1,0:T(8,128)(2,1)} %constant.16.clone.cos_ref) | copy-start | bytes 7077892
  0.0 32.5 %copy-start.1 = (bf16[1024,1024]{1,0:T(8,128)(2,1)S(1)}, bf16[1024,1024]{1,0:T(8,128)(2,1)}, u32[]{:S(2)}) copy-start(bf16[1024,1024]{1,0:T(8,128)(2,1)} %constant.17.clone.sin_ref) | copy-start | bytes 6291460
  0.0 32.5 %copy-start.7 = (bf16[256,128]{1,0:T(8,128)(2,1)S(1)}, bf16[256,128]{1,0:T(8,128)(2,1)}, u32[]{:S(2)}) copy-start(bf16[256,128]{1,0:T(8,128)(2,1)} %constant.20.clone.flip_ref) | copy-start | bytes 196612
  0.0 32.5 %copy-start.8 = (s32[1024]{0:T(1024)S(1)}, s32[1024]{0:T(1024)}, u32[]{:S(2)}) copy-start(s32[1024]{0:T(1024)} %param.14) | copy-start | bytes 12292
  0.0 32.5 %copy-start.9 = (s32[1024]{0:T(1024)S(1)}, s32[1024]{0:T(1024)}, u32[]{:S(2)}) copy-start(s32[1024]{0:T(1024)} %param.15) | copy-start | bytes 12292
  32.5 26.6 %copy-start.2 = (bf16[1024,896]{1,0:T(8,128)(2,1)S(1)}, bf16[1024,896]{1,0:T(8,128)(2,1)}, u32[]{:S(2)}) copy-start(bf16[1024,896]{1,0:T(8,128)(2,1)} %constant.19.clone.sin_ref) | copy-start | bytes 5505028
  32.5 26.6 %copy-start.3 = (bf16[1024,768]{1,0:T(8,128)(2,1)S(1)}, bf16[1024,768]{1,0:T(8,128)(2,1)}, u32[]{:S(2)}) copy-start(bf16[1024,768]{1,0:T(8,128)(2,1)} %constant.18.clone.cos_ref) | copy-start | bytes 4718596
  32.5 26.6 %copy-start.4 = (bf16[640,512]{1,0:T(8,128)(2,1)S(1)}, bf16[640,512]{1,0:T(8,128)(2,1)}, u32[]{:S(2)}) copy-start(bf16[640,512]{1,0:T(8,128)(2,1)} %constant.22.clone.mirror_ref) | copy-start | bytes 1966084
  32.5 26.6 %copy-start.5 = (bf16[512,512]{1,0:T(8,128)(2,1)S(1)}, bf16[512,512]{1,0:T(8,128)(2,1)}, u32[]{:S(2)}) copy-start(bf16[512,512]{1,0:T(8,128)(2,1)} %constant.21.clone.lead_ref) | copy-start | bytes 1572868
  32.5 26.6 %copy-start.6 = (bf16[128,512]{1,0:T(8,128)(2,1)S(1)}, bf16[128,512]{1,0:T(8,128)(2,1)}, u32[]{:S(2)}) copy-start(bf16[128,512]{1,0:T(8,128)(2,1)} %constant.23.clone.middle_ref) | copy-start | bytes 393220

commit v4 on v3

--- a/solution.py
+++ b/solution.py
@@ -49,13 +49,13 @@
     cos_y, sin_y = mode_tables(NY, NN)
     half = N_GY // 2
     cos_rows = np.zeros((half, 32, 768), np.float32)
-    sin_rows = np.zeros((half, 32, 896), np.float32)
+    sin_rows = np.zeros((half, 32, 768), np.float32)
     cos_rows[:, :ROWS_Y, :NN] = cos_y[: half * ROWS_Y].reshape(half, ROWS_Y, NN)
     cos_rows[0, ROWS_Y, :NN] = cos_y[half * ROWS_Y]
-    sin_rows[:, :ROWS_Y, 96 : 96 + NN] = sin_y[: half * ROWS_Y].reshape(half, ROWS_Y, NN)
+    sin_rows[:, :ROWS_Y, :NN] = sin_y[: half * ROWS_Y].reshape(half, ROWS_Y, NN)
     return (
         cos_rows.reshape(half * 32, 768).astype(BF16),
-        sin_rows.reshape(half * 32, 896).astype(BF16),
+        sin_rows.reshape(half * 32, 768).astype(BF16),
     )
 
 
@@ -68,7 +68,6 @@
 
 
 def y_selections():
-    lead = np.zeros((4 * LANE, 4 * LANE), np.float32)
     mirror = np.zeros((5 * LANE, 4 * LANE), np.float32)
     middle = np.zeros((LANE, 4 * LANE), np.float32)
     for g in range(4):
@@ -76,12 +75,11 @@
         for u in range(4):
             for j in range(ROWS_Y):
                 n = LANE * g + 32 * u + j
-                lead[LANE * u + 32 * g + j, n] = 1.0
                 if j:
                     mirror[LANE * (3 - u) + 32 * g + ROWS_Y - j, n] = 1.0
                 else:
                     mirror[LANE * (4 - u) + 32 * g, n] = 1.0
-    return lead.astype(BF16), mirror.astype(BF16), middle.astype(BF16)
+    return mirror.astype(BF16), middle.astype(BF16)
 
 
 def iota(shape, dim):
@@ -179,7 +177,7 @@
 
 
 def y_kernel(
-    got_ref, own_ref, cos_ref, sin_ref, lead_ref, mirror_ref, middle_ref, out_hbm, wide_ref, out_ref, sems
+    got_ref, own_ref, cos_ref, sin_ref, mirror_ref, middle_ref, out_hbm, wide_ref, out_ref, sems
 ):
     half = N_GY // 2
     groups = half // 4
@@ -196,7 +194,15 @@
         ],
         0,
     )
-    lead = dot(lead, lead_ref[...])
+    lead = jnp.concatenate(
+        [
+            jnp.concatenate(
+                [got[4 * t + u][:, 32 * g : 32 * g + 32] for g in range(4) for u in range(4)], 1
+            )
+            for t in range(groups)
+        ],
+        0,
+    ).astype(F32)
     mirror = dot(back, mirror_ref[...])
     middle = dot(got[half], middle_ref[...])
     even = lead + mirror
@@ -218,9 +224,7 @@
     odd = rows_of(odd)
     sin_part = dot(odd, sin_ref[...])
     cos_part = dot(even, cos_ref[...])
-    both = jnp.concatenate(
-        [cos_part[:, :640], cos_part[:, 640:] + sin_part[:, :LANE], sin_part[:, LANE:]], 1
-    )[:, : 2 * NN]
+    both = jnp.concatenate([cos_part[:, :NN], sin_part[:, :NN]], 1)
     lane = iota((MCAP, 2 * NN), 1)
     lane = jnp.where(lane >= NN, lane - NN, lane)
     keep = lane < own_ref[:, 0:1]

time: 61.2 us -> 61.1 us (level)
  no operation moved by 1% of the time
where the time goes in v4:
time: 61.1 us; the launch traced here: 60.8 us
  blocking collectives  55.9 us (91%)
  Pallas kernels  4.82 us (8%)
    all_to_all x1, blocking collectives, body(): lax.all_to_all(ordered, 'gx', split_axis=0, concat_axis=0, tiled=True)  31.2 us
    all_to_all x1, blocking collectives, body(): lax.all_to_all(outgoing, 'gy', split_axis=0, concat_axis=0, tiled=True)  24.7 us
    pallas_call x1, Pallas kernels, x_transform(): pl.pallas_call(x_kernel, out_shape=(pltpu.VMEM((N_GY * HALF, LANE), BF16)...  1.88 us
    pallas_call x1, Pallas kernels, y_transform(): pl.pallas_call(y_kernel, out_shape=jax.ShapeDtypeStruct((1, MCAP, 4 * NN)...  1.71 us
    pallas_call x1, Pallas kernels, order_levels(): pl.pallas_call(order_kernel, out_shape=pltpu.VMEM((N_GX, 24, LANE), BF16)...  1.23 us

profile of v4, /device:TPU:1, one launch (start us, length us, event | category | flops | bytes accessed | tf_op | source)
XLA Modules:
  0.0 60.8 jit_solution(18328391961811064127)
XLA Ops:
  0.0 0.0 copy-start
  0.0 0.0 copy-start.1
  0.0 0.0 copy-start.6
  0.0 0.0 copy-start.7
  0.0 0.0 copy-start.8
  0.0 1.2 %order_levels.1 = bf16[16,24,128]{2,1,0:T(8,128)(2,1)S(1)} custom-call(s32[1,16]{1,0:T(1,128)} %bitcast.11, bf16[23,16,128]{2,1,0:T(8,128)(2,1)} %bitcast.10), custom_call_target="tpu_custom_call" | custom-call | flops 4000000000 | bytes 100000 | tf_op jit(solution)/shard_map/order_levels/pallas_call | solution.py:277
  1.3 31.2 %all_to_all.10.grid_ref = bf16[16,24,128]{2,1,0:T(8,128)(2,1)S(1)} all-to-all(bf16[16,24,128]{2,1,0:T(8,128)(2,1)S(1)} %order_levels.1), channel_id=1, replica_groups=mesh['gy'=64,'gx'=16] {'gx'}, dimensions={0} | all-to-all | bytes 196608 | tf_op jit(solution)/shard_map/all_to_all | solution.py:329
  32.5 0.0 copy-done
  32.5 0.0 copy-done.1
  32.5 0.0 copy-done.6
  32.5 0.0 copy-done.7
  32.5 0.0 copy-done.8
  32.5 0.0 copy-start.2
  32.5 0.0 copy-start.3
  32.5 0.0 copy-start.4
  32.5 0.0 copy-start.5
  32.5 1.9 %x_transform.1 = (bf16[768,128]{1,0:T(8,128)(2,1)S(1)}, s32[24,128]{1,0:T(8,128)S(1)}) custom-call(bf16[16,24,128]{2,1,0:T(8,128)(2,1)S(1)} %all_to_all.10.grid_ref, s32[1,1024]{1,0:T(1,128)S(1)} %bitcast.8, s32[1,1024]{1,0:T(1,128)S(1)} %bitcast.9, bf16[1152,1024]{1,0:T(8,128)(2,1)S(1)} %copy-done, bf16[1024,1024]{1,0:T(8,128)(2,1)S(1)} %copy-done.1, ...), custom_call_target="tpu_custom_call" | custom-call | tf_op jit(solution)/shard_map/x_transform/pallas_call | solution.py:295
  34.4 24.7 %all_to_all.11 = bf16[192,4,128]{2,1,0:T(4,128)(2,1)S(1)} all-to-all(bf16[192,4,128]{2,1,0:T(4,128)(2,1)S(1)} %bitcast.7), channel_id=1, replica_groups=mesh['gy'=64,'gx'=16] {'gy'}, dimensions={0} | all-to-all | bytes 393216 | tf_op jit(solution)/shard_map/all_to_all | solution.py:332
  59.1 0.0 copy-done.2
  59.1 0.0 copy-done.3
  59.1 0.0 copy-done.4
  59.1 0.0 copy-done.5
  59.1 1.7 %y_transform.1 = f32[1,24,2944]{2,1,0:T(8,128)} custom-call(bf16[768,128]{1,0:T(8,128)(2,1)S(1)} %bitcast.6, s32[24,128]{1,0:T(8,128)S(1)} %get-tuple-element.8.own_ref, bf16[1024,768]{1,0:T(8,128)(2,1)S(1)} %copy-done.3, bf16[1024,768]{1,0:T(8,128)(2,1)S(1)} %copy-done.2, bf16[640,512]{1,0:T(8,128)(2,1)S(1)} %copy-done.4, bf16[128,512]{1,0:T(8,128)(2,1)S(1)} %copy-done.5), custom_call_target="tpu_custom_call" | custom-call | tf_op jit(solution)/shard_map/y_transform/pallas_call | solution.py:310
Async XLA Ops:
  0.0 32.5 %copy-start = (bf16[1152,1024]{1,0:T(8,128)(2,1)S(1)}, bf16[1152,1024]{1,0:T(8,128)(2,1)}, u32[]{:S(2)}) copy-start(bf16[1152,1024]{1,0:T(8,128)(2,1)} %constant.14.clone.cos_ref) | copy-start | bytes 7077892
  0.0 32.5 %copy-start.1 = (bf16[1024,1024]{1,0:T(8,128)(2,1)S(1)}, bf16[1024,1024]{1,0:T(8,128)(2,1)}, u32[]{:S(2)}) copy-start(bf16[1024,1024]{1,0:T(8,128)(2,1)} %constant.15.clone.sin_ref) | copy-start | bytes 6291460
  0.0 32.5 %copy-start.6 = (bf16[256,128]{1,0:T(8,128)(2,1)S(1)}, bf16[256,128]{1,0:T(8,128)(2,1)}, u32[]{:S(2)}) copy-start(bf16[256,128]{1,0:T(8,128)(2,1)} %constant.18.clone.flip_ref) | copy-start | bytes 196612
  0.0 32.5 %copy-start.7 = (s32[1024]{0:T(1024)S(1)}, s32[1024]{0:T(1024)}, u32[]{:S(2)}) copy-start(s32[1024]{0:T(1024)} %param.13) | copy-start | bytes 12292
  0.0 32.5 %copy-start.8 = (s32[1024]{0:T(1024)S(1)}, s32[1024]{0:T(1024)}, u32[]{:S(2)}) copy-start(s32[1024]{0:T(1024)} %param.14) | copy-start | bytes 12292
  32.5 26.6 %copy-start.2 = (bf16[1024,768]{1,0:T(8,128)(2,1)S(1)}, bf16[1024,768]{1,0:T(8,128)(2,1)}, u32[]{:S(2)}) copy-start(bf16[1024,768]{1,0:T(8,128)(2,1)} %constant.17.clone.sin_ref) | copy-start | bytes 4718596
  32.5 26.6 %copy-start.3 = (bf16[1024,768]{1,0:T(8,128)(2,1)S(1)}, bf16[1024,768]{1,0:T(8,128)(2,1)}, u32[]{:S(2)}) copy-start(bf16[1024,768]{1,0:T(8,128)(2,1)} %constant.16.clone.cos_ref) | copy-start | bytes 4718596
  32.5 26.6 %copy-start.4 = (bf16[640,512]{1,0:T(8,128)(2,1)S(1)}, bf16[640,512]{1,0:T(8,128)(2,1)}, u32[]{:S(2)}) copy-start(bf16[640,512]{1,0:T(8,128)(2,1)} %constant.19.clone.mirror_ref) | copy-start | bytes 1966084
  32.5 26.6 %copy-start.5 = (bf16[128,512]{1,0:T(8,128)(2,1)S(1)}, bf16[128,512]{1,0:T(8,128)(2,1)}, u32[]{:S(2)}) copy-start(bf16[128,512]{1,0:T(8,128)(2,1)} %constant.20.clone.middle_ref) | copy-start | bytes 393220

commit v5 on v4

--- a/solution.py
+++ b/solution.py
@@ -68,10 +68,9 @@
 
 
 def y_selections():
-    mirror = np.zeros((5 * LANE, 4 * LANE), np.float32)
-    middle = np.zeros((LANE, 4 * LANE), np.float32)
+    mirror = np.zeros((6 * LANE, 4 * LANE), np.float32)
     for g in range(4):
-        middle[32 * g, LANE * g + ROWS_Y] = 1.0
+        mirror[LANE * 5 + 32 * g, LANE * g + ROWS_Y] = 2.0
         for u in range(4):
             for j in range(ROWS_Y):
                 n = LANE * g + 32 * u + j
@@ -79,7 +78,7 @@
                     mirror[LANE * (3 - u) + 32 * g + ROWS_Y - j, n] = 1.0
                 else:
                     mirror[LANE * (4 - u) + 32 * g, n] = 1.0
-    return mirror.astype(BF16), middle.astype(BF16)
+    return (mirror.astype(BF16),)
 
 
 def iota(shape, dim):
@@ -177,7 +176,7 @@
 
 
 def y_kernel(
-    got_ref, own_ref, cos_ref, sin_ref, mirror_ref, middle_ref, out_hbm, wide_ref, out_ref, sems
+    got_ref, own_ref, cos_ref, sin_ref, mirror_ref, out_hbm, wide_ref, out_ref, sems
 ):
     half = N_GY // 2
     groups = half // 4
@@ -187,9 +186,12 @@
     lead = jnp.concatenate(
         [jnp.concatenate([got[4 * t + u] for u in range(4)], 1) for t in range(groups)], 0
     )
+    none = jnp.zeros((16, LANE), BF16)
     back = jnp.concatenate(
         [
-            jnp.concatenate([got[(60 - 4 * t + v) % N_GY] for v in range(5)], 1)
+            jnp.concatenate(
+                [got[(60 - 4 * t + v) % N_GY] for v in range(5)] + [none if t else got[half]], 1
+            )
             for t in range(groups)
         ],
         0,
@@ -204,10 +206,9 @@
         0,
     ).astype(F32)
     mirror = dot(back, mirror_ref[...])
-    middle = dot(got[half], middle_ref[...])
     even = lead + mirror
     odd = (lead - mirror).astype(BF16)
-    even = jnp.concatenate([even[:16] + 2.0 * middle, even[16:]], 0).astype(BF16)
+    even = even.astype(BF16)
 
     def rows_of(v):
         return jnp.concatenate(

time: 61.1 us -> 61 us (level)
  no operation moved by 1% of the time
where the time goes in v5:
time: 61 us; the launch traced here: 60.8 us
  blocking collectives  55.9 us (92%)
  Pallas kernels  4.81 us (8%)
    all_to_all x1, blocking collectives, body(): lax.all_to_all(ordered, 'gx', split_axis=0, concat_axis=0, tiled=True)  31.2 us
    all_to_all x1, blocking collectives, body(): lax.all_to_all(outgoing, 'gy', split_axis=0, concat_axis=0, tiled=True)  24.7 us
    pallas_call x1, Pallas kernels, x_transform(): pl.pallas_call(x_kernel, out_shape=(pltpu.VMEM((N_GY * HALF, LANE), BF16)...  1.88 us
    pallas_call x1, Pallas kernels, y_transform(): pl.pallas_call(y_kernel, out_shape=jax.ShapeDtypeStruct((1, MCAP, 4 * NN)...  1.7 us
    pallas_call x1, Pallas kernels, order_levels(): pl.pallas_call(order_kernel, out_shape=pltpu.VMEM((N_GX, 24, LANE), BF16)...  1.23 us

profile of v5, /device:TPU:1, one launch (start us, length us, event | category | flops | bytes accessed | tf_op | source)
XLA Modules:
  0.0 60.8 jit_solution(5129616014524295081)
XLA Ops:
  0.0 0.0 copy-start
  0.0 0.0 copy-start.1
  0.0 0.0 copy-start.5
  0.0 0.0 copy-start.6
  0.0 0.0 copy-start.7
  0.0 1.2 %order_levels.1 = bf16[16,24,128]{2,1,0:T(8,128)(2,1)S(1)} custom-call(s32[1,16]{1,0:T(1,128)} %bitcast.11, bf16[23,16,128]{2,1,0:T(8,128)(2,1)} %bitcast.10), custom_call_target="tpu_custom_call" | custom-call | flops 4000000000 | bytes 100000 | tf_op jit(solution)/shard_map/order_levels/pallas_call | solution.py:278
  1.3 31.2 %all_to_all.10.grid_ref = bf16[16,24,128]{2,1,0:T(8,128)(2,1)S(1)} all-to-all(bf16[16,24,128]{2,1,0:T(8,128)(2,1)S(1)} %order_levels.1), channel_id=1, replica_groups=mesh['gy'=64,'gx'=16] {'gx'}, dimensions={0} | all-to-all | bytes 196608 | tf_op jit(solution)/shard_map/all_to_all | solution.py:330
  32.5 0.0 copy-done
  32.5 0.0 copy-done.1
  32.5 0.0 copy-done.5
  32.5 0.0 copy-done.6
  32.5 0.0 copy-done.7
  32.5 0.0 copy-start.2
  32.5 0.0 copy-start.3
  32.5 0.0 copy-start.4
  32.5 1.9 %x_transform.1 = (bf16[768,128]{1,0:T(8,128)(2,1)S(1)}, s32[24,128]{1,0:T(8,128)S(1)}) custom-call(bf16[16,24,128]{2,1,0:T(8,128)(2,1)S(1)} %all_to_all.10.grid_ref, s32[1,1024]{1,0:T(1,128)S(1)} %bitcast.8, s32[1,1024]{1,0:T(1,128)S(1)} %bitcast.9, bf16[1152,1024]{1,0:T(8,128)(2,1)S(1)} %copy-done, bf16[1024,1024]{1,0:T(8,128)(2,1)S(1)} %copy-done.1, ...), custom_call_target="tpu_custom_call" | custom-call | tf_op jit(solution)/shard_map/x_transform/pallas_call | solution.py:296
  34.4 24.7 %all_to_all.11 = bf16[192,4,128]{2,1,0:T(4,128)(2,1)S(1)} all-to-all(bf16[192,4,128]{2,1,0:T(4,128)(2,1)S(1)} %bitcast.7), channel_id=1, replica_groups=mesh['gy'=64,'gx'=16] {'gy'}, dimensions={0} | all-to-all | bytes 393216 | tf_op jit(solution)/shard_map/all_to_all | solution.py:333
  59.1 0.0 copy-done.2
  59.1 0.0 copy-done.3
  59.1 0.0 copy-done.4
  59.1 1.7 %y_transform.1 = f32[1,24,2944]{2,1,0:T(8,128)} custom-call(bf16[768,128]{1,0:T(8,128)(2,1)S(1)} %bitcast.6, s32[24,128]{1,0:T(8,128)S(1)} %get-tuple-element.8.own_ref, bf16[1024,768]{1,0:T(8,128)(2,1)S(1)} %copy-done.3, bf16[1024,768]{1,0:T(8,128)(2,1)S(1)} %copy-done.2, bf16[768,512]{1,0:T(8,128)(2,1)S(1)} %copy-done.4), custom_call_target="tpu_custom_call" | custom-call | tf_op jit(solution)/shard_map/y_transform/pallas_call | solution.py:311
Async XLA Ops:
  0.0 32.5 %copy-start = (bf16[1152,1024]{1,0:T(8,128)(2,1)S(1)}, bf16[1152,1024]{1,0:T(8,128)(2,1)}, u32[]{:S(2)}) copy-start(bf16[1152,1024]{1,0:T(8,128)(2,1)} %constant.12.clone.cos_ref) | copy-start | bytes 7077892
  0.0 32.5 %copy-start.1 = (bf16[1024,1024]{1,0:T(8,128)(2,1)S(1)}, bf16[1024,1024]{1,0:T(8,128)(2,1)}, u32[]{:S(2)}) copy-start(bf16[1024,1024]{1,0:T(8,128)(2,1)} %constant.13.clone.sin_ref) | copy-start | bytes 6291460
  0.0 32.5 %copy-start.5 = (bf16[256,128]{1,0:T(8,128)(2,1)S(1)}, bf16[256,128]{1,0:T(8,128)(2,1)}, u32[]{:S(2)}) copy-start(bf16[256,128]{1,0:T(8,128)(2,1)} %constant.16.clone.flip_ref) | copy-start | bytes 196612
  0.0 32.5 %copy-start.6 = (s32[1024]{0:T(1024)S(1)}, s32[1024]{0:T(1024)}, u32[]{:S(2)}) copy-start(s32[1024]{0:T(1024)} %param.12) | copy-start | bytes 12292
  0.0 32.5 %copy-start.7 = (s32[1024]{0:T(1024)S(1)}, s32[1024]{0:T(1024)}, u32[]{:S(2)}) copy-start(s32[1024]{0:T(1024)} %param.13) | copy-start | bytes 12292
  32.5 26.6 %copy-start.2 = (bf16[1024,768]{1,0:T(8,128)(2,1)S(1)}, bf16[1024,768]{1,0:T(8,128)(2,1)}, u32[]{:S(2)}) copy-start(bf16[1024,768]{1,0:T(8,128)(2,1)} %constant.15.clone.sin_ref) | copy-start | bytes 4718596
  32.5 26.6 %copy-start.3 = (bf16[1024,768]{1,0:T(8,128)(2,1)S(1)}, bf16[1024,768]{1,0:T(8,128)(2,1)}, u32[]{:S(2)}) copy-start(bf16[1024,768]{1,0:T(8,128)(2,1)} %constant.14.clone.cos_ref) | copy-start | bytes 4718596
  32.5 26.6 %copy-start.4 = (bf16[768,512]{1,0:T(8,128)(2,1)S(1)}, bf16[768,512]{1,0:T(8,128)(2,1)}, u32[]{:S(2)}) copy-start(bf16[768,512]{1,0:T(8,128)(2,1)} %constant.17.clone.mirror_ref) | copy-start | bytes 2359300
